TPU v7x, 128 devices: a whole 4x4x4 slice. The times are simulated.
128 devices in a mesh: grp: 8 (over x, core), row: 16 (over y, z).
Axes of the slice: x: 4, y: 4, z: 4, core: 2. Of those that a mesh axis runs over, the one named last changes fastest.
Arguments:
- table: float32 [16, 131072, 128], P('grp', 'row'), may hold values from -6 to 6
- row_shard: int32 [16, 32768, 1], P('grp'), may hold values from 0 to 15; in each aligned block of 256 rows (0 to 255, 256 to 511, ..., all dimensions but the last counted through in order) at most 48 rows name the same one
- row_offset: int32 [16, 32768], P('grp'), may hold values from 0 to 8191
- bag_lengths: int32 [16, 128, 128], P('grp'), may hold values from 1 to 4, 256 in all within a row
Outputs:
- pooled: float32 [16, 16384, 128], P(None, ('grp', 'row'))
Inputs may be any that keep to these rules, and one draw needn't show every extreme that they name: `row_shard`: in each aligned block of 256 lookups of a table (the lookups of one block of bags), at most 48 lookups name the same row shard, and in every draw some block reaches 48. `bag_lengths`: the 128 lengths of each block sum to 256.
All inputs are finite; a program needn't handle non-finite values.
Results may differ from a plain program's by a relative error of at most 0.0003.
Values sent between devices are 32-bit elements; how exact they have to be, the bound alone decides.
No kernel may reach another device: no remote copies, remote signals or barrier semaphores. Data moves between devices by JAX's collectives and lax.ppermute only.
A program may use at most 64 MiB of HBM per device.

v0:
```python
import jax
import jax.numpy as jnp
from jax import lax
from jax.sharding import Mesh
from jax.sharding import PartitionSpec as P

GRP = ("grp_0", "grp_1")
GRP_ROW = ("grp_0", "grp_1", "row")


def cut_along(array, dim, count):
    shape = array.shape
    pieces = array.reshape(*shape[:dim], count, shape[dim] // count, *shape[dim + 1 :])
    return jnp.moveaxis(pieces, dim, 0)


def laid_out(pieces, dim):
    shape = list(pieces.shape[1:])
    shape[dim] *= pieces.shape[0]
    return jnp.moveaxis(pieces, 0, dim).reshape(shape)


def moved_by_axis(pieces, axes, turns):
    inside = pieces.shape[1:]
    whole = pieces.reshape(*(lax.axis_size(a) for a in axes), *inside)
    for k in turns:
        whole = lax.all_to_all(whole, axes[k], k, k, tiled=True)
    return whole.reshape(-1, *inside)


def exchange_by_axis(array, axes, turns, split_dim, concat_dim):
    pieces = cut_along(array, split_dim, lax.axis_size(axes))
    return laid_out(moved_by_axis(pieces, axes, turns), concat_dim)


def grouped_exchange(array, axis, split_dim, concat_dim, work, item_dim, out_dim):
    items = jax.tree.leaves(array)[0].shape[item_dim]
    count = 2 if items % 2 == 0 else 1
    outs = []
    for k in range(count):
        group = jax.tree.map(
            lambda a: lax.slice_in_dim(
                a, k * (items // count), (k + 1) * (items // count), axis=item_dim
            ),
            array,
        )
        outs.append(
            work(
                lax.all_to_all(
                    group, axis, split_axis=split_dim, concat_axis=concat_dim, tiled=True
                )
            )
        )
    return jax.tree.map(lambda *parts: jnp.concatenate(parts, axis=out_dim), *outs)


def bag_weights(lengths, look_block):
    ends = jnp.cumsum(lengths, axis=-1)
    starts = ends - lengths
    places = lax.broadcasted_iota(jnp.int32, lengths.shape + (look_block,), lengths.ndim)
    inside = (places >= starts[..., None]) & (places < ends[..., None])
    return inside.astype(jnp.float32)


def fetch_rows(table, index):
    flat = index.reshape(index.shape[0], -1)
    picked = jax.vmap(lambda matrix, wanted: jnp.take(matrix, wanted, axis=0))(table, flat)
    return picked.reshape(index.shape + (table.shape[-1],))


def to_owners(pooled, bags_block, width):
    moved = exchange_by_axis(pooled, GRP, (1, 0), 1, 0)
    return moved.reshape(moved.shape[0], bags_block, width)


def body(table, row_shard, row_offset, bag_lengths):
    groups = lax.axis_size(GRP)
    shards = lax.axis_size("row")
    mine = lax.axis_index("row")
    tables_here = table.shape[0]
    width = table.shape[2]
    bags_block = bag_lengths.shape[2]
    look_block = row_offset.shape[1] // (groups * shards)
    capacity = 3 * look_block // shards
    owner = row_shard.reshape(tables_here, groups, shards, look_block)
    offset = row_offset.reshape(tables_here, groups, shards, look_block)
    lengths = bag_lengths.reshape(tables_here, groups, shards, bags_block)
    owner_own = lax.dynamic_index_in_dim(owner, mine, 2, keepdims=False)
    offset_own = lax.dynamic_index_in_dim(offset, mine, 2, keepdims=False)
    length_own = lax.dynamic_index_in_dim(lengths, mine, 2, keepdims=False)
    targets = lax.broadcasted_iota(jnp.int32, owner_own.shape + (shards,), 3)
    hits = (owner_own[..., None] == targets).astype(jnp.int32)
    before = jnp.cumsum(hits, axis=2) - hits
    slot = jnp.sum(before * hits, axis=3)
    slots = lax.broadcasted_iota(jnp.int32, (capacity,), 0)
    match = (hits[..., None] == 1) & (slot[..., None, None] == slots)
    requests = jnp.sum(jnp.where(match, offset_own[..., None, None], 0), axis=2)

    def serve(asked):
        found = fetch_rows(table, asked)
        return lax.all_to_all(found, "row", split_axis=2, concat_axis=2, tiled=True)

    returned = grouped_exchange(requests, "row", 2, 2, serve, 3, 3)
    flat = returned.reshape(tables_here, groups, shards * capacity, width)
    chosen = match.astype(jnp.float32).reshape(tables_here, groups, look_block, shards * capacity)
    weights = bag_weights(length_own, look_block)
    slot_weights = jnp.einsum("tgbl,tglk->tgbk", weights, chosen, precision=lax.Precision.HIGHEST)
    pooled = jnp.einsum("tgbk,tgke->tgbe", slot_weights, flat, precision=lax.Precision.HIGHEST)
    return to_owners(pooled, bags_block, width)


def solution(mesh):
    torus = Mesh(mesh.devices.reshape(4, 2, mesh.shape["row"]), ("grp_0", "grp_1", "row"))
    placed = (P(GRP, "row", None), P(GRP, None, None), P(GRP, None), P(GRP, None, None))
    return jax.shard_map(
        body, mesh=torus, in_specs=placed, out_specs=P(None, GRP_ROW, None), check_vma=False
    )
```

profile of v0, /device:TPU:0, one launch (start us, length us, event | category | flops | bytes accessed | tf_op | source)
XLA Modules:
  0.0 618.1 jit_solution(17247412002378588777)
XLA Ops:
  0.0 1.7 reduce
  2.9 9.1 %reduce-window.6 = s32[2,8,16,2,128]{4,2,3,1,0:T(8,128)S(1)} reduce-window(s32[2,8,16,2,128]{4,2,3,1,0:T(8,128)S(1)} %fusion.7, s32[]{:T(128)} %constant.32.clone.1), window={size=1x1x1x1x128 pad=0_0x0_0x0_0x0_0x127_0}, to_apply=%region_1.2 | reduce-window | flops 8323072 | bytes 524292 | tf_op jit(solution)/shard_map/reduce-window
  12.8 4.4 select_reduce_fusion
  18.1 8.2 %all-to-all-start.2 = ((s32[16,1,384]{2,1,0:T(1,128)}), s32[16,1,384]{2,1,0:T(1,128)S(1)}, u32[]{:S(2)}, u32[]{:S(2)}) async-start(s32[16,1,384]{2,1,0:T(1,128)} %reshape.121), calls=%async_computation.2 | async-start | bytes 49152 | tf_op jit(solution)/shard_map/all_to_all | solution.py:49
  27.0 6.8 %all-to-all-done.2 = s32[16,1,384]{2,1,0:T(1,128)S(1)} async-done(((s32[16,1,384]{2,1,0:T(1,128)}), s32[16,1,384]{2,1,0:T(1,128)S(1)}, u32[]{:S(2)}, u32[]{:S(2)}) %all-to-all-start.2) | async-done | bytes 24608 | tf_op jit(solution)/shard_map/all_to_all | solution.py:49
  33.9 3.5 all-to-all-start
  39.0 251.9 %gather_fusion.1 = f32[6144,128]{1,0:T(8,128)S(1)} fusion(f32[2,8192,128]{2,1,0:T(8,128)} %param.6, s32[6144]{0:T(1024)S(1)} %bitcast.75), kind=kCustom, calls=%fused_computation.1.clone | custom fusion | bytes 6340608 | tf_op jit(solution)/shard_map/vmap(jit(_take))/gather | solution.py:67
  290.9 1.1 broadcast_select_fusion
  292.0 2.1 copy.43
  294.1 11.6 %all-to-all-start.3 = ((f32[2,8,16,24,128]{4,3,1,0,2:T(8,128)}), f32[2,8,16,24,128]{4,3,1,0,2:T(8,128)S(1)}, u32[]{:S(2)}, u32[]{:S(2)}) async-start(f32[2,8,16,24,128]{4,3,1,0,2:T(8,128)} %copy.43), calls=%async_computation.3 | async-start | bytes 6291456 | tf_op jit(solution)/shard_map/all_to_all | solution.py:101
  307.1 1.6 copy.39
  308.7 1.0 reshape.81
  309.8 102.1 %gather_fusion = f32[6144,128]{1,0:T(8,128)} fusion(f32[2,8192,128]{2,1,0:T(8,128)} %param.6, s32[6144]{0:T(1024)S(1)} %bitcast.76), kind=kCustom, calls=%fused_computation.clone | custom fusion | bytes 6340608 | tf_op jit(solution)/shard_map/vmap(jit(_take))/gather | solution.py:67
  412.0 3.2 broadcast_select_fusion.1
  415.2 2.1 copy.40
  417.3 126.0 %all-to-all-start.1 = ((f32[2,8,16,24,128]{4,3,1,0,2:T(8,128)}), f32[2,8,16,24,128]{4,3,1,0,2:T(8,128)}, u32[]{:S(2)}, u32[]{:S(2)}) async-start(f32[2,8,16,24,128]{4,3,1,0,2:T(8,128)} %copy.40), calls=%async_computation.1 | async-start | bytes 6291456 | tf_op jit(solution)/shard_map/all_to_all | solution.py:101
  543.9 1.8 broadcast_and_fusion
  545.7 4.3 fusion.1
  549.9 30.4 %all-to-all-done.1 = f32[2,8,16,24,128]{4,3,1,0,2:T(8,128)} async-done(((f32[2,8,16,24,128]{4,3,1,0,2:T(8,128)}), f32[2,8,16,24,128]{4,3,1,0,2:T(8,128)}, u32[]{:S(2)}, u32[]{:S(2)}) %all-to-all-start.1) | async-done | bytes 3145760 | tf_op jit(solution)/shard_map/all_to_all | solution.py:101
  580.4 2.6 pad_maximum_fusion
  584.7 6.6 %fusion.13 = f32[2,8,128,128]{3,2,1,0:T(8,128)S(1)} fusion(f32[2,8,128,768]{3,2,1,0:T(8,128)S(1)} %bitcast.78, f32[2,8,768,128]{3,2,1,0:T(8,128)S(1)} %bitcast.79), kind=kOutput, calls=%fused_computation.42 | convolution fusion | flops 2415919104 | bytes 13631488 | tf_op jit(solution)/shard_map/tgbk,tgke->tgbe/dot_general | solution.py:108
  591.4 4.6 all_to_all.30
  596.0 21.0 %all_to_all.31 = f32[4,2,2,1,128,128]{5,4,1,2,3,0:T(8,128)S(1)} all-to-all(f32[4,2,2,1,128,128]{5,4,1,2,3,0:T(8,128)S(1)} %copy.46), channel_id=1, replica_groups=mesh['grp_0'=4,'grp_1'=2,'row'=16] {'grp_0'}, dimensions={0} | all-to-all | bytes 2097152 | tf_op jit(solution)/shard_map/all_to_all | solution.py:27
  617.1 1.1 copy.47
  (51 shorter events, 9.1 us)
Async XLA Ops:
  0.0 543.2 %copy-start = (s32[2,128,128]{2,1,0:T(8,128)S(1)}, s32[2,128,128]{2,1,0:T(8,128)}, u32[]{:S(2)}) copy-start(s32[2,128,128]{2,1,0:T(8,128)} %param.9) | copy-start | bytes 393220
  2.8 36.1 %copy-start.1 = (pred[2,8,256,16]{2,3,1,0:T(8,128)(4,1)}, pred[2,8,256,16]{2,3,1,0:T(8,128)(4,1)S(1)}, u32[]{:S(2)}) copy-start(pred[2,8,256,16]{2,3,1,0:T(8,128)(4,1)S(1)} %convert_compare_fusion) | copy-start | bytes 196612
  18.1 15.8 %all-to-all-start.2 = ((s32[16,1,384]{2,1,0:T(1,128)}), s32[16,1,384]{2,1,0:T(1,128)S(1)}, u32[]{:S(2)}, u32[]{:S(2)}) async-start(s32[16,1,384]{2,1,0:T(1,128)} %reshape.121), calls=%async_computation.2 | async-start | bytes 49152 | tf_op jit(solution)/shard_map/all_to_all | solution.py:49
  33.9 260.2 %all-to-all-start = ((s32[16,1,384]{2,1,0:T(1,128)}), s32[16,1,384]{2,1,0:T(1,128)S(1)}, u32[]{:S(2)}, u32[]{:S(2)}) async-start(s32[16,1,384]{2,1,0:T(1,128)} %reshape.123), calls=%async_computation | async-start | bytes 49152 | tf_op jit(solution)/shard_map/all_to_all | solution.py:49
  294.1 123.2 %all-to-all-start.3 = ((f32[2,8,16,24,128]{4,3,1,0,2:T(8,128)}), f32[2,8,16,24,128]{4,3,1,0,2:T(8,128)S(1)}, u32[]{:S(2)}, u32[]{:S(2)}) async-start(f32[2,8,16,24,128]{4,3,1,0,2:T(8,128)} %copy.43), calls=%async_computation.3 | async-start | bytes 6291456 | tf_op jit(solution)/shard_map/all_to_all | solution.py:101
  417.3 126.6 %copy-start.2 = (pred[2,8,256,16]{2,3,1,0:T(8,128)(4,1)S(1)}, pred[2,8,256,16]{2,3,1,0:T(8,128)(4,1)}, u32[]{:S(2)}) copy-start(pred[2,8,256,16]{2,3,1,0:T(8,128)(4,1)} %copy-done.1) | copy-start | bytes 196612
  417.3 163.1 %all-to-all-start.1 = ((f32[2,8,16,24,128]{4,3,1,0,2:T(8,128)}), f32[2,8,16,24,128]{4,3,1,0,2:T(8,128)}, u32[]{:S(2)}, u32[]{:S(2)}) async-start(f32[2,8,16,24,128]{4,3,1,0,2:T(8,128)} %copy.40), calls=%async_computation.1 | async-start | bytes 6291456 | tf_op jit(solution)/shard_map/all_to_all | solution.py:101
  580.4 3.3 slice-start
  583.0 1.7 slice-start.1
where the time goes:
time: 624 us; the launch traced here: 618 us
  local copies, waits for them, and re-layouts  368 us (59%)
  starting transfers between devices  149 us (24%)
  waiting for transfers between devices  37.3 us (6%)
  other arithmetic  26.5 us (4%)
  blocking collectives  25.6 us (4%)
  matrix products  10.8 us (2%)
    gather x2, local copies, waits for them, and re-layouts, fetch_rows(): jnp.take(matrix, wanted, axis=0)  354 us
    all_to_all x2, starting transfers between devices, serve(): return lax.all_to_all(found, 'row', split_axis=2, concat_axis=2, tiled=True)  138 us
    all_to_all x2, waiting for transfers between devices, serve(): return lax.all_to_all(found, 'row', split_axis=2, concat_axis=2, tiled=True)  30.4 us
    all_to_all x2, blocking collectives, moved_by_axis(): whole = lax.all_to_all(whole, axes[k], k, k, tiled=True)  25.6 us
  transfers between devices with their start and end apart: 4, of which 2 were waited for; matrix products, arithmetic and copies ran while one was open for 61% of the time, Pallas kernels for 0%

commit v1 on v0

v1 whole, which is shorter than its diff:
```python
import functools

import jax
import jax.numpy as jnp
from jax import lax
from jax.experimental import pallas as pl
from jax.experimental.pallas import tpu as pltpu
from jax.sharding import PartitionSpec as P

AXES = ("grp", "row")
F32 = jnp.float32
BF16 = jnp.bfloat16
NT = (((1,), (1,)), ((), ()))
VMEM_LIMIT = 56 * 1024 * 1024


def list_kernel(cap, me_ref, shard_ref, offset_ref, list_ref, key_s, off_s):
    tables, blocks, look = shard_ref.shape
    me = me_ref[0]
    later = lax.broadcasted_iota(jnp.int32, (look, look), 0)
    earlier = lax.broadcasted_iota(jnp.int32, (look, look), 1)
    tri = (earlier < later).astype(F32).astype(BF16)
    places = [(lax.broadcasted_iota(jnp.int32, (8, blocks), 0) + 8 * i).astype(F32) for i in range(cap // 8)]
    for t in range(tables):
        hit = (shard_ref[t] == me).astype(F32)
        rank = lax.dot_general(tri, hit.astype(BF16), NT, preferred_element_type=F32)
        key_s[...] = jnp.where(jnp.transpose(hit) > 0.5, rank, -1.0)
        off_s[...] = jnp.transpose(offset_ref[t].astype(F32))

        def step(i, accs):
            for u in range(8):
                key = key_s[pl.ds(i * 8 + u, 1), :]
                off = off_s[pl.ds(i * 8 + u, 1), :]
                accs = tuple(jnp.where(key == pos, off, acc) for acc, pos in zip(accs, places))
            return accs

        accs = lax.fori_loop(0, look // 8, step, tuple(jnp.zeros((8, blocks), F32) for _ in places))
        for i, acc in enumerate(accs):
            list_ref[t, pl.ds(8 * i, 8), :] = acc.astype(jnp.int32)


def make_lists(me, shard, offset, cap):
    tables, blocks, look = shard.shape
    return pl.pallas_call(
        functools.partial(list_kernel, cap),
        out_shape=jax.ShapeDtypeStruct((tables, cap, blocks), jnp.int32),
        in_specs=[
            pl.BlockSpec(memory_space=pltpu.SMEM),
            pl.BlockSpec(memory_space=pltpu.VMEM),
            pl.BlockSpec(memory_space=pltpu.VMEM),
        ],
        out_specs=pl.BlockSpec(memory_space=pltpu.VMEM),
        scratch_shapes=[pltpu.VMEM((look, blocks), F32), pltpu.VMEM((look, blocks), F32)],
        cost_estimate=pl.CostEstimate(flops=20_000_000, bytes_accessed=600_000, transcendentals=0),
        name="lists",
    )(me, shard, offset)


def gather_kernel(cap, per_step, list_ref, table_ref, out_ref):
    first = pl.program_id(0) * per_step

    def one(k, carry):
        for j in range(cap):
            row = list_ref[j, first + k]
            out_ref[pl.ds(k * cap + j, 1), :] = table_ref[0, pl.ds(row, 1), :]
        return carry

    lax.fori_loop(0, per_step, one, 0)


def gather_rows(lists, table, t, steps):
    cap, blocks = lists.shape
    _, rows, width = table.shape
    per_step = blocks // steps
    return pl.pallas_call(
        functools.partial(gather_kernel, cap, per_step),
        grid=(steps,),
        out_shape=jax.ShapeDtypeStruct((blocks * cap, width), F32),
        in_specs=[
            pl.BlockSpec(memory_space=pltpu.SMEM),
            pl.BlockSpec((1, rows, width), lambda i: (t, 0, 0)),
        ],
        out_specs=pl.BlockSpec((per_step * cap, width), lambda i: (i, 0)),
        compiler_params=pltpu.CompilerParams(vmem_limit_bytes=VMEM_LIMIT),
        cost_estimate=pl.CostEstimate(flops=40_000_000, bytes_accessed=8_000_000, transcendentals=0),
        name="gather",
    )(lists, table)


def weight_kernel(cap, shards, shard_ref, length_ref, out_ref):
    look = shard_ref.shape[2]
    bags = length_ref.shape[2]
    shard = shard_ref[0].astype(F32)
    ids = lax.broadcasted_iota(jnp.int32, (shards, look), 0).astype(F32)
    hit = (shard == ids).astype(F32)
    row = lax.broadcasted_iota(jnp.int32, (look, look), 0)
    col = lax.broadcasted_iota(jnp.int32, (look, look), 1)
    upper = (row < col).astype(F32).astype(BF16)
    before = jnp.dot(hit.astype(BF16), upper, preferred_element_type=F32)
    slot = jnp.sum(hit * before, axis=0, keepdims=True) + shard * cap
    places = lax.broadcasted_iota(jnp.int32, (shards * cap, look), 0).astype(F32)
    chosen = (places == slot).astype(F32).astype(BF16)
    brow = lax.broadcasted_iota(jnp.int32, (bags, bags), 0)
    bcol = lax.broadcasted_iota(jnp.int32, (bags, bags), 1)
    length = length_ref[0].astype(F32)
    ends = jnp.sum(jnp.where(bcol <= brow, length, 0.0), axis=1, keepdims=True)
    starts = jnp.sum(jnp.where(bcol < brow, length, 0.0), axis=1, keepdims=True)
    spot = lax.broadcasted_iota(jnp.int32, (bags, look), 1).astype(F32)
    inside = ((spot >= starts) & (spot < ends)).astype(F32).astype(BF16)
    out_ref[0] = lax.dot_general(inside, chosen, NT, preferred_element_type=F32).astype(BF16)


def make_weights(shard, length, cap, shards):
    tables, _, look = shard.shape
    bags = length.shape[2]
    return pl.pallas_call(
        functools.partial(weight_kernel, cap, shards),
        grid=(tables,),
        out_shape=jax.ShapeDtypeStruct((tables, bags, shards * cap), BF16),
        in_specs=[
            pl.BlockSpec((1, 1, look), lambda i: (i, 0, 0)),
            pl.BlockSpec((1, 1, bags), lambda i: (i, 0, 0)),
        ],
        out_specs=pl.BlockSpec((1, bags, shards * cap), lambda i: (i, 0, 0)),
        cost_estimate=pl.CostEstimate(flops=30_000_000, bytes_accessed=3_000_000, transcendentals=0),
        name="weights",
    )(shard, length)


def pool_kernel(weight_ref, rows_ref, out_ref):
    rows = rows_ref[0]
    high = rows.astype(BF16)
    low = (rows - high.astype(F32)).astype(BF16)
    weight = weight_ref[0, 0]
    out_ref[0, 0] = jnp.dot(weight, high, preferred_element_type=F32) + jnp.dot(
        weight, low, preferred_element_type=F32
    )


def pool_kernel_into(weight_ref, rows_ref, held_ref, out_ref):
    pool_kernel(weight_ref, rows_ref, out_ref)


def pool(weights, rows, t, held):
    groups, per_group, bags, slots = weights.shape
    width = rows.shape[2]
    in_specs = [
        pl.BlockSpec((1, 1, bags, slots), lambda i: (i, t, 0, 0)),
        pl.BlockSpec((1, slots, width), lambda i: (i, 0, 0)),
    ]
    args = [weights, rows]
    if held is not None:
        in_specs.append(pl.BlockSpec(memory_space=pl.ANY))
        args.append(held)
    return pl.pallas_call(
        pool_kernel if held is None else pool_kernel_into,
        grid=(groups,),
        out_shape=jax.ShapeDtypeStruct((groups, per_group, bags, width), F32),
        in_specs=in_specs,
        out_specs=pl.BlockSpec((1, 1, bags, width), lambda i: (i, t, 0, 0)),
        input_output_aliases={} if held is None else {2: 0},
        cost_estimate=pl.CostEstimate(flops=20_000_000, bytes_accessed=4_000_000, transcendentals=0),
        name="pool",
    )(*args)


def body(table, row_shard, row_offset, bag_lengths):
    groups = lax.axis_size("grp")
    shards = lax.axis_size("row")
    mine = lax.axis_index("row")
    tables, _, width = table.shape
    blocks, bags = bag_lengths.shape[1:]
    look = row_offset.shape[1] // blocks
    cap = 3 * look // shards
    shard = row_shard.reshape(tables, blocks, look)
    offset = row_offset.reshape(tables, blocks, look)

    per_owner = (tables, groups, shards)
    own = jnp.concatenate(
        [
            lax.dynamic_index_in_dim(shard.reshape(*per_owner, look), mine, 2, keepdims=False),
            lax.dynamic_index_in_dim(bag_lengths.reshape(*per_owner, bags), mine, 2, keepdims=False),
        ],
        axis=2,
    )
    about = lax.all_to_all(own.transpose(1, 0, 2), "grp", 0, 0, tiled=True)
    about = about.reshape(groups * tables, 1, look + bags)
    weights = make_weights(about[..., :look], about[..., look:], cap, shards)
    weights = weights.reshape(groups, tables, bags, shards * cap)

    lists = make_lists(mine.reshape(1), shard, offset, cap)
    moved = []
    for t in range(tables):
        rows = gather_rows(lists[t], table, t, 8).reshape(blocks, cap, width)
        moved.append(lax.all_to_all(rows, AXES, 0, 0, tiled=True))
    out = None
    for t in range(tables):
        out = pool(weights, moved[t].reshape(groups, shards * cap, width), t, out)
    return out.reshape(groups * tables, bags, width)


def solution(mesh):
    placed = (P("grp", "row", None), P("grp", None, None), P("grp", None), P("grp", None, None))
    return jax.shard_map(
        body, mesh=mesh, in_specs=placed, out_specs=P(None, AXES, None), check_vma=False
    )
```

time: 624 us -> 133 us (0.21)
  local copies, waits for them, and re-layouts: 368 us -> 6.91 us
  starting transfers between devices: 149 us -> 21.7 us
  Pallas kernels: 0 us -> 48.6 us
  blocking collectives: 25.6 us -> 0 us
  other arithmetic: 26.5 us -> 2.35 us
  waiting for transfers between devices: 37.3 us -> 52.1 us
  matrix products: 10.8 us -> 0 us
    gather x2 -> x0, local copies, waits for them, and re-layouts: 354 us -> none  [fetch_rows(): jnp.take(matrix, wanted, axis=0)]
    all_to_all x4 -> x3, starting transfers between devices: 149 us -> 21.7 us  [the longest x2 17.3 us: body(): moved.append(lax.all_to_all(rows, AXES, 0, 0, tiled=True))]
    pallas_call x0 -> x6, Pallas kernels: none -> 48.6 us  [the longest x2 20.9 us: gather_rows(): pl.pallas_call(functools.partial(gather_kernel, cap, per_step), grid=(ste...]
    all_to_all x2 -> x0, blocking collectives: 25.6 us -> none  [moved_by_axis(): whole = lax.all_to_all(whole, axes[k], k, k, tiled=True)]
    all_to_all x4 -> x3, waiting for transfers between devices: 37.3 us -> 52.1 us  [the longest x2 52.1 us: body(): moved.append(lax.all_to_all(rows, AXES, 0, 0, tiled=True))]
    dot_general x2 -> x0, matrix products: 10.8 us -> none  [the longest x1 6.56 us: body(): jnp.einsum('tgbk,tgke->tgbe', slot_weights, flat, precision=lax.Precision...]
    another operation x3 -> x0, other arithmetic: 9.8 us -> none
  transfers between devices with their start and end apart: 4 -> 3, of which waited for: 2 -> 2; matrix products, arithmetic and copies ran while one was open for 61% -> 3% of each run, Pallas kernels for 0% -> 32%
where the time goes in v1:
time: 133 us; the launch traced here: 132 us
  waiting for transfers between devices  52.1 us (39%)
  Pallas kernels  48.6 us (37%)
  starting transfers between devices  21.7 us (16%)
  local copies, waits for them, and re-layouts  6.91 us (5%)
  other arithmetic  2.35 us (2%)
    all_to_all x2, waiting for transfers between devices, body(): moved.append(lax.all_to_all(rows, AXES, 0, 0, tiled=True))  52.1 us
    pallas_call x2, Pallas kernels, gather_rows(): pl.pallas_call(functools.partial(gather_kernel, cap, per_step), grid=(ste...  20.9 us
    all_to_all x2, starting transfers between devices, body(): moved.append(lax.all_to_all(rows, AXES, 0, 0, tiled=True))  17.3 us
    pallas_call x2, Pallas kernels, pool(): pl.pallas_call(pool_kernel if held is None else pool_kernel_into, grid=(g...  13.6 us
    pallas_call x1, Pallas kernels, make_weights(): pl.pallas_call(functools.partial(weight_kernel, cap, shards), grid=(table...  11 us
    all_to_all x1, starting transfers between devices, body(): about = lax.all_to_all(own.transpose(1, 0, 2), 'grp', 0, 0, tiled=True)  4.41 us
    unnamed x7, local copies, waits for them, and re-layouts  4.23 us
    pallas_call x1, Pallas kernels, make_lists(): pl.pallas_call(functools.partial(list_kernel, cap), out_shape=jax.ShapeDt...  3.2 us
  transfers between devices with their start and end apart: 3, of which 2 were waited for; matrix products, arithmetic and copies ran while one was open for 3% of the time, Pallas kernels for 32%

profile of v1, /device:TPU:0, one launch (start us, length us, event | category | flops | bytes accessed | tf_op | source)
XLA Modules:
  0.0 131.7 jit_solution(12172194456800998116)
XLA Ops:
  0.0 0.0 copy-start
  0.0 0.9 copy-done
  0.9 1.7 %reduce = s32[2,32768]{1,0:T(2,128)S(1)} reduce(s32[2,32768,1]{1,2,0:T(1,128)} %param.5, s32[]{:T(128)} %constant.7.clone.1), dimensions={2}, to_apply=%param.5.reduce_sub_computation | reduce | bytes 524292 | tf_op args[1]
  2.7 0.0 copy-start.2
  2.7 0.6 add_bitcast_fusion
  3.4 4.4 %all-to-all-start = ((s32[8,2,384]{2,1,0:T(2,128)}), s32[8,2,384]{2,1,0:T(2,128)S(1)}, u32[]{:S(2)}, u32[]{:S(2)}) async-start(s32[8,2,384]{2,1,0:T(2,128)} %add_bitcast_fusion), calls=%async_computation | async-start | bytes 49152 | tf_op jit(solution)/shard_map/all_to_all | solution.py:186
  7.8 1.7 %copy.16 = s32[1,2,128,256]{3,2,1,0:T(8,128)} copy(s32[1,2,128,256]{3,1,2,0:T(2,128)} %bitcast.41) | data formatting | bytes 524288
  9.5 0.0 copy-done.2
  9.5 3.2 %lists.1 = s32[2,48,128]{2,1,0:T(8,128)} custom-call(s32[1]{0:T(128)} %bitcast.5.me_ref, s32[2,128,256]{2,1,0:T(8,128)} %bitcast.38, s32[2,128,256]{2,1,0:T(8,128)} %bitcast.40), custom_call_target="tpu_custom_call" | custom-call | flops 20000000 | bytes 600000 | tf_op jit(solution)/shard_map/lists/pallas_call | solution.py:44
  12.7 1.4 %slice_bitcast_fusion = (s32[48,128]{1,0:T(8,128)}, s32[48,128]{1,0:T(8,128)}) fusion(s32[2,48,128]{2,1,0:T(8,128)} %lists.1), kind=kLoop, calls=%fused_computation.1 | loop fusion | bytes 98304 | tf_op jit(solution)/shard_map/squeeze | solution.py:194
  14.0 10.4 %gather.3 = f32[6144,128]{1,0:T(8,128)} custom-call(s32[48,128]{1,0:T(8,128)} %get-tuple-element.7.list_ref, f32[2,8192,128]{2,1,0:T(8,128)} %table_ref.3), custom_call_target="tpu_custom_call" | custom-call | flops 40000000 | bytes 8000000 | tf_op jit(solution)/shard_map/gather/pallas_call | solution.py:75
  24.4 0.0 all-to-all-done
  24.4 11.6 %all-to-all-start.2 = ((f32[128,48,128]{2,1,0:T(8,128)}), f32[128,48,128]{2,1,0:T(8,128)S(1)}, u32[]{:S(2)}, u32[]{:S(2)}) async-start(f32[128,48,128]{2,1,0:T(8,128)} %bitcast.36), calls=%async_computation.2 | async-start | bytes 6291456 | tf_op jit(solution)/shard_map/all_to_all | solution.py:195
  36.0 10.5 %gather.2 = f32[6144,128]{1,0:T(8,128)} custom-call(s32[48,128]{1,0:T(8,128)} %get-tuple-element.8.list_ref, f32[2,8192,128]{2,1,0:T(8,128)} %table_ref.3), custom_call_target="tpu_custom_call" | custom-call | flops 40000000 | bytes 8000000 | tf_op jit(solution)/shard_map/gather/pallas_call | solution.py:75
  46.5 30.5 %all-to-all-done.2 = f32[128,48,128]{2,1,0:T(8,128)S(1)} async-done(((f32[128,48,128]{2,1,0:T(8,128)}), f32[128,48,128]{2,1,0:T(8,128)S(1)}, u32[]{:S(2)}, u32[]{:S(2)}) %all-to-all-start.2) | async-done | bytes 3145760 | tf_op jit(solution)/shard_map/all_to_all | solution.py:195
  77.0 0.0 copy-start.1
  77.0 1.6 %copy-done.1 = f32[128,48,128]{2,1,0:T(8,128)} copy-done((f32[128,48,128]{2,1,0:T(8,128)}, f32[128,48,128]{2,1,0:T(8,128)S(1)}, u32[]{:S(2)}) %copy-start.1) | copy-done | bytes 3145752
  78.6 5.7 %all-to-all-start.1 = ((f32[128,48,128]{2,1,0:T(8,128)}), f32[128,48,128]{2,1,0:T(8,128)}, u32[]{:S(2)}, u32[]{:S(2)}) async-start(f32[128,48,128]{2,1,0:T(8,128)} %bitcast.35), calls=%async_computation.1 | async-start | bytes 6291456 | tf_op jit(solution)/shard_map/all_to_all | solution.py:195
  84.4 0.6 slice.17.length_ref
  85.0 0.6 slice.16.shard_ref
  85.6 11.0 %weights.1 = bf16[16,128,768]{2,1,0:T(8,128)(2,1)} custom-call(s32[16,1,256]{2,1,0:T(1,128)} %slice.16.shard_ref, s32[16,1,128]{2,1,0:T(1,128)} %slice.17.length_ref), custom_call_target="tpu_custom_call" | custom-call | flops 30000000 | bytes 3000000 | tf_op jit(solution)/shard_map/weights/pallas_call | solution.py:116
  96.6 6.8 %pool.2.held_ref = f32[8,2,128,128]{3,2,1,0:T(8,128)} custom-call(bf16[8,2,128,768]{3,2,1,0:T(8,128)(2,1)} %bitcast.32, f32[8,768,128]{2,1,0:T(8,128)} %bitcast.34), custom_call_target="tpu_custom_call" | custom-call | flops 20000000 | bytes 4000000 | tf_op jit(solution)/shard_map/pool/pallas_call | solution.py:155
  103.4 21.5 %all-to-all-done.1 = f32[128,48,128]{2,1,0:T(8,128)} async-done(((f32[128,48,128]{2,1,0:T(8,128)}), f32[128,48,128]{2,1,0:T(8,128)}, u32[]{:S(2)}, u32[]{:S(2)}) %all-to-all-start.1) | async-done | bytes 3145760 | tf_op jit(solution)/shard_map/all_to_all | solution.py:195
  124.9 6.8 %pool.3 = f32[8,2,128,128]{3,2,1,0:T(8,128)} custom-call(bf16[8,2,128,768]{3,2,1,0:T(8,128)(2,1)} %bitcast.33, f32[8,768,128]{2,1,0:T(8,128)} %bitcast.8.rows_ref, f32[8,2,128,128]{3,2,1,0:T(8,128)} %pool.2.held_ref), custom_call_target="tpu_custom_call", output_to_operand_aliasing={{}: (2, {})} | custom-call | flops 20000000 | bytes 4000000 | tf_op jit(solution)/shard_map/pool/pallas_call | solution.py:155
  (6 shorter events, 0.1 us)
Async XLA Ops:
  0.0 0.9 copy-start
  2.7 6.8 %copy-start.2 = (s32[1,2,128,256]{3,2,1,0:T(8,128)}, s32[1,2,128,256]{3,2,1,0:T(8,128)S(1)}, u32[]{:S(2)}) copy-start(s32[1,2,128,256]{3,2,1,0:T(8,128)S(1)} %copy.19) | copy-start | bytes 786436
  3.4 21.1 %all-to-all-start = ((s32[8,2,384]{2,1,0:T(2,128)}), s32[8,2,384]{2,1,0:T(2,128)S(1)}, u32[]{:S(2)}, u32[]{:S(2)}) async-start(s32[8,2,384]{2,1,0:T(2,128)} %add_bitcast_fusion), calls=%async_computation | async-start | bytes 49152 | tf_op jit(solution)/shard_map/all_to_all | solution.py:186
  24.4 52.5 %all-to-all-start.2 = ((f32[128,48,128]{2,1,0:T(8,128)}), f32[128,48,128]{2,1,0:T(8,128)S(1)}, u32[]{:S(2)}, u32[]{:S(2)}) async-start(f32[128,48,128]{2,1,0:T(8,128)} %bitcast.36), calls=%async_computation.2 | async-start | bytes 6291456 | tf_op jit(solution)/shard_map/all_to_all | solution.py:195
  77.0 1.7 %copy-start.1 = (f32[128,48,128]{2,1,0:T(8,128)}, f32[128,48,128]{2,1,0:T(8,128)S(1)}, u32[]{:S(2)}) copy-start(f32[128,48,128]{2,1,0:T(8,128)S(1)} %all-to-all-done.2) | copy-start | bytes 9437188
  78.6 46.3 %all-to-all-start.1 = ((f32[128,48,128]{2,1,0:T(8,128)}), f32[128,48,128]{2,1,0:T(8,128)}, u32[]{:S(2)}, u32[]{:S(2)}) async-start(f32[128,48,128]{2,1,0:T(8,128)} %bitcast.35), calls=%async_computation.1 | async-start | bytes 6291456 | tf_op jit(solution)/shard_map/all_to_all | solution.py:195

commit v2 on v1

v2 whole, which is shorter than its diff:
```python
import functools

import jax
import jax.numpy as jnp
from jax import lax
from jax.experimental import pallas as pl
from jax.experimental.pallas import tpu as pltpu
from jax.sharding import PartitionSpec as P

AXES = ("grp", "row")
F32 = jnp.float32
BF16 = jnp.bfloat16
NT = (((1,), (1,)), ((), ()))
VMEM_LIMIT = 56 * 1024 * 1024
LANES = 128
PIECES = 8


def front_kernel(tables, blocks, cap, me_ref, shard_ref, offset_ref, table_ref, out_ref,
                 key_s, off_s, list_v, list_s, held, rows, table_sem, list_sem, out_sem):
    look = key_s.shape[0]
    halves = look // LANES
    size = table_ref.shape[1]
    me = me_ref[0]
    fetch = [
        pltpu.make_async_copy(table_ref.at[t], held.at[pl.ds(t * size, size)], table_sem.at[t])
        for t in range(tables)
    ]
    for copy in fetch:
        copy.start()
    later = lax.broadcasted_iota(jnp.int32, (look, look), 0)
    earlier = lax.broadcasted_iota(jnp.int32, (look, look), 1)
    tri = (earlier < later).astype(F32).astype(BF16)
    places = [(lax.broadcasted_iota(jnp.int32, (8, blocks), 0) + 8 * i).astype(F32) for i in range(cap // 8)]
    for t in range(tables):
        hit = jnp.concatenate(
            [(shard_ref[t, pl.ds(h, blocks, stride=halves), :] == me).astype(F32) for h in range(halves)], axis=1
        )
        rank = lax.dot_general(tri, hit.astype(BF16), NT, preferred_element_type=F32)
        key_s[...] = jnp.where(jnp.transpose(hit) > 0.5, rank, -1.0)
        for h in range(halves):
            off = offset_ref[pl.ds(h * tables + t, blocks, stride=halves * tables), :] + t * size
            off_s[pl.ds(h * LANES, LANES), :] = jnp.transpose(off.astype(F32))

        def step(i, accs):
            for u in range(8):
                key = key_s[pl.ds(i * 8 + u, 1), :]
                off = off_s[pl.ds(i * 8 + u, 1), :]
                accs = tuple(jnp.where(key == pos, off, acc) for acc, pos in zip(accs, places))
            return accs

        accs = lax.fori_loop(0, look // 8, step, tuple(jnp.zeros((8, blocks), F32) for _ in places))
        whole = jnp.concatenate(list(accs) + [jnp.zeros((LANES - cap, blocks), F32)], axis=0)
        list_v[pl.ds(t * blocks, blocks), :] = jnp.transpose(whole).astype(jnp.int32)
    listed = pltpu.make_async_copy(list_v, list_s, list_sem)
    listed.start()
    listed.wait()
    for copy in fetch:
        copy.wait()

    per_piece = blocks // PIECES
    per_block = tables * cap

    def block(k, carry):
        for t in range(tables):
            for j in range(cap):
                row = list_s[t * blocks + k, j]
                rows[pl.ds(k * per_block + t * cap + j, 1), :] = held[pl.ds(row, 1), :]
        return carry

    sends = []
    for i in range(PIECES):
        lax.fori_loop(i * per_piece, (i + 1) * per_piece, block, 0)
        part = pl.ds(i * per_piece * per_block, per_piece * per_block)
        copy = pltpu.make_async_copy(rows.at[part], out_ref.at[part], out_sem.at[i])
        copy.start()
        sends.append(copy)
    for copy in sends:
        copy.wait()


def front(me, shard, offset, table, blocks, cap):
    tables, size, width = table.shape
    look = shard.shape[1] * LANES // blocks
    return pl.pallas_call(
        functools.partial(front_kernel, tables, blocks, cap),
        out_shape=jax.ShapeDtypeStruct((blocks * tables * cap, width), F32),
        in_specs=[
            pl.BlockSpec(memory_space=pltpu.SMEM),
            pl.BlockSpec(memory_space=pltpu.VMEM),
            pl.BlockSpec(memory_space=pltpu.VMEM),
            pl.BlockSpec(memory_space=pl.ANY),
        ],
        out_specs=pl.BlockSpec(memory_space=pl.ANY),
        scratch_shapes=[
            pltpu.VMEM((look, blocks), F32),
            pltpu.VMEM((look, blocks), F32),
            pltpu.VMEM((tables * blocks, LANES), jnp.int32),
            pltpu.SMEM((tables * blocks, LANES), jnp.int32),
            pltpu.VMEM((tables * size, width), F32),
            pltpu.VMEM((blocks * tables * cap, width), F32),
            pltpu.SemaphoreType.DMA((tables,)),
            pltpu.SemaphoreType.DMA,
            pltpu.SemaphoreType.DMA((PIECES,)),
        ],
        compiler_params=pltpu.CompilerParams(vmem_limit_bytes=VMEM_LIMIT),
        cost_estimate=pl.CostEstimate(flops=60_000_000, bytes_accessed=15_000_000, transcendentals=0),
        name="front",
    )(me, shard, offset, table)


def weight_kernel(cap, shards, shard_ref, length_ref, out_ref):
    look = shard_ref.shape[2]
    bags = length_ref.shape[2]
    shard = shard_ref[0].astype(F32)
    ids = lax.broadcasted_iota(jnp.int32, (shards, look), 0).astype(F32)
    hit = (shard == ids).astype(F32)
    row = lax.broadcasted_iota(jnp.int32, (look, look), 0)
    col = lax.broadcasted_iota(jnp.int32, (look, look), 1)
    upper = (row < col).astype(F32).astype(BF16)
    before = jnp.dot(hit.astype(BF16), upper, preferred_element_type=F32)
    slot = jnp.sum(hit * before, axis=0, keepdims=True) + shard * cap
    places = lax.broadcasted_iota(jnp.int32, (shards * cap, look), 0).astype(F32)
    chosen = (places == slot).astype(F32).astype(BF16)
    brow = lax.broadcasted_iota(jnp.int32, (bags, bags), 0)
    bcol = lax.broadcasted_iota(jnp.int32, (bags, bags), 1)
    length = length_ref[0].astype(F32)
    ends = jnp.sum(jnp.where(bcol <= brow, length, 0.0), axis=1, keepdims=True)
    starts = jnp.sum(jnp.where(bcol < brow, length, 0.0), axis=1, keepdims=True)
    spot = lax.broadcasted_iota(jnp.int32, (bags, look), 1).astype(F32)
    inside = ((spot >= starts) & (spot < ends)).astype(F32).astype(BF16)
    out_ref[0] = lax.dot_general(inside, chosen, NT, preferred_element_type=F32).astype(BF16)


def make_weights(shard, length, cap, shards):
    tables, _, look = shard.shape
    bags = length.shape[2]
    return pl.pallas_call(
        functools.partial(weight_kernel, cap, shards),
        grid=(tables,),
        out_shape=jax.ShapeDtypeStruct((tables, bags, shards * cap), BF16),
        in_specs=[
            pl.BlockSpec((1, 1, look), lambda i: (i, 0, 0)),
            pl.BlockSpec((1, 1, bags), lambda i: (i, 0, 0)),
        ],
        out_specs=pl.BlockSpec((1, bags, shards * cap), lambda i: (i, 0, 0)),
        cost_estimate=pl.CostEstimate(flops=30_000_000, bytes_accessed=3_000_000, transcendentals=0),
        name="weights",
    )(shard, length)


def pool_kernel(tables, cap, weight_ref, rows_ref, out_ref):
    shards, _, width = rows_ref.shape
    for t in range(tables):
        rows = rows_ref[:, pl.ds(t * cap, cap), :].reshape(shards * cap, width)
        high = rows.astype(BF16)
        low = (rows - high.astype(F32)).astype(BF16)
        both = jnp.dot(weight_ref[t], jnp.concatenate([high, low], axis=1), preferred_element_type=F32)
        out_ref[t] = both[:, :width] + both[:, width:]


def pool(weights, rows, groups, cap):
    total, bags, slots = weights.shape
    tables = total // groups
    shards = rows.shape[0] // groups
    width = rows.shape[2]
    return pl.pallas_call(
        functools.partial(pool_kernel, tables, cap),
        grid=(groups,),
        out_shape=jax.ShapeDtypeStruct((total, bags, width), F32),
        in_specs=[
            pl.BlockSpec((tables, bags, slots), lambda i: (i, 0, 0)),
            pl.BlockSpec((shards, tables * cap, width), lambda i: (i, 0, 0)),
        ],
        out_specs=pl.BlockSpec((tables, bags, width), lambda i: (i, 0, 0)),
        cost_estimate=pl.CostEstimate(flops=20_000_000, bytes_accessed=4_000_000, transcendentals=0),
        name="pool",
    )(weights, rows)


def body(table, row_shard, row_offset, bag_lengths):
    groups = lax.axis_size("grp")
    shards = lax.axis_size("row")
    mine = lax.axis_index("row")
    tables, _, width = table.shape
    blocks, bags = bag_lengths.shape[1:]
    lookups = row_offset.shape[1]
    look = lookups // blocks
    cap = 3 * look // shards

    shard = row_shard.reshape(tables, lookups // LANES, LANES)
    offset = row_offset.reshape(tables, lookups // LANES, LANES).transpose(1, 0, 2)
    rows = front(mine.reshape(1), shard, offset.reshape(-1, LANES), table, blocks, cap)
    moved = lax.all_to_all(rows.reshape(blocks, tables * cap, width), AXES, 0, 0, tiled=True)

    per_owner = (tables, groups, shards)
    own = jnp.concatenate(
        [
            lax.dynamic_index_in_dim(row_shard.reshape(*per_owner, look), mine, 2, keepdims=False),
            lax.dynamic_index_in_dim(bag_lengths.reshape(*per_owner, bags), mine, 2, keepdims=False),
        ],
        axis=2,
    )
    about = lax.all_to_all(own.transpose(1, 0, 2), "grp", 0, 0, tiled=True)
    about = about.reshape(groups * tables, 1, look + bags)
    weights = make_weights(about[..., :look], about[..., look:], cap, shards)
    return pool(weights, moved, groups, cap)


def solution(mesh):
    placed = (P("grp", "row", None), P("grp", None, None), P("grp", None), P("grp", None, None))
    return jax.shard_map(
        body, mesh=mesh, in_specs=placed, out_specs=P(None, AXES, None), check_vma=False
    )
```

time: 133 us -> 125 us (0.940)
  waiting for transfers between devices: 52.1 us -> 68.2 us
  Pallas kernels: 48.6 us -> 35.4 us
  starting transfers between devices: 21.7 us -> 16.4 us
  local copies, waits for them, and re-layouts: 6.91 us -> 2.23 us
    all_to_all x2 -> x1, waiting for transfers between devices: 52.1 us -> 68.2 us  [body(): lax.all_to_all(rows.reshape(blocks, tables * cap, width), AXES, 0, 0, til...]
    pallas_call x5 -> x2, Pallas kernels: 37.7 us -> 24.5 us  [the longest x1 16.6 us: front(): pl.pallas_call(functools.partial(front_kernel, tables, blocks, cap), out_...]
    all_to_all x2 -> x1, starting transfers between devices: 17.3 us -> 12 us  [body(): lax.all_to_all(rows.reshape(blocks, tables * cap, width), AXES, 0, 0, til...]
    unnamed x7 -> x3, local copies, waits for them, and re-layouts: 4.23 us -> 0.92 us
    squeeze x1 -> x0, local copies, waits for them, and re-layouts: 1.37 us -> none  [body(): rows = gather_rows(lists[t], table, t, 8).reshape(blocks, cap, width)]
  transfers between devices with their start and end apart: 3 -> 2, of which waited for: 2 -> 1; matrix products, arithmetic and copies ran while one was open for 3% -> 1% of each run, Pallas kernels for 32% -> 22%
where the time goes in v2:
time: 125 us
  waiting for transfers between devices  68.2 us (55%)
  Pallas kernels  35.4 us (28%)
  starting transfers between devices  16.4 us (13%)
  other arithmetic  2.33 us (2%)
  local copies, waits for them, and re-layouts  2.23 us (2%)
    all_to_all x1, waiting for transfers between devices, body(): lax.all_to_all(rows.reshape(blocks, tables * cap, width), AXES, 0, 0, til...  68.2 us
    pallas_call x1, Pallas kernels, front(): pl.pallas_call(functools.partial(front_kernel, tables, blocks, cap), out_...  16.6 us
    all_to_all x1, starting transfers between devices, body(): lax.all_to_all(rows.reshape(blocks, tables * cap, width), AXES, 0, 0, til...  12 us
    pallas_call x1, Pallas kernels, make_weights(): pl.pallas_call(functools.partial(weight_kernel, cap, shards), grid=(table...  11 us
    pallas_call x1, Pallas kernels, pool(): pl.pallas_call(functools.partial(pool_kernel, tables, cap), grid=(groups,...  7.82 us
    all_to_all x1, starting transfers between devices, body(): about = lax.all_to_all(own.transpose(1, 0, 2), 'grp', 0, 0, tiled=True)  4.41 us
  transfers between devices with their start and end apart: 2, of which 1 were waited for; matrix products, arithmetic and copies ran while one was open for 1% of the time, Pallas kernels for 22%

profile of v2, /device:TPU:0, one launch (start us, length us, event | category | flops | bytes accessed | tf_op | source)
XLA Modules:
  0.0 124.7 jit_solution(17312227574469337266)
XLA Ops:
  0.0 0.0 copy-start
  0.0 0.9 copy-done
  0.9 1.7 %reduce = s32[2,32768]{1,0:T(2,128)S(1)} reduce(s32[2,32768,1]{1,2,0:T(1,128)} %param.5, s32[]{:T(128)} %constant.7.clone.1), dimensions={2}, to_apply=%param.5.reduce_sub_computation | reduce | bytes 524292 | tf_op args[1]
  2.7 0.6 add_bitcast_fusion
  3.3 4.4 %all-to-all-start = ((s32[8,2,384]{2,1,0:T(2,128)}), s32[8,2,384]{2,1,0:T(2,128)S(1)}, u32[]{:S(2)}, u32[]{:S(2)}) async-start(s32[8,2,384]{2,1,0:T(2,128)} %add_bitcast_fusion), calls=%async_computation | async-start | bytes 49152 | tf_op jit(solution)/shard_map/all_to_all | solution.py:204
  7.8 16.6 %front.1 = f32[12288,128]{1,0:T(8,128)} custom-call(s32[1]{0:T(128)} %bitcast.4.me_ref, s32[2,256,128]{2,1,0:T(8,128)} %bitcast.22, s32[512,128]{1,0:T(8,128)} %bitcast.25, f32[2,8192,128]{2,1,0:T(8,128)} %table_ref.1), custom_call_target="tpu_custom_call" | custom-call | flops 60000000 | bytes 15000000 | tf_op jit(solution)/shard_map/front/pallas_call | solution.py:85
  24.4 0.0 all-to-all-done
  24.4 12.0 %all-to-all-start.1 = ((f32[128,96,128]{2,1,0:T(8,128)}), f32[128,96,128]{2,1,0:T(8,128)}, u32[]{:S(2)}, u32[]{:S(2)}) async-start(f32[128,96,128]{2,1,0:T(8,128)} %bitcast.21), calls=%async_computation.1 | async-start | bytes 12582912 | tf_op jit(solution)/shard_map/all_to_all | solution.py:194
  36.5 0.6 slice.9.length_ref
  37.1 0.6 slice.8.shard_ref
  37.7 11.0 %weights.1.weight_ref = bf16[16,128,768]{2,1,0:T(8,128)(2,1)} custom-call(s32[16,1,256]{2,1,0:T(1,128)} %slice.8.shard_ref, s32[16,1,128]{2,1,0:T(1,128)} %slice.9.length_ref), custom_call_target="tpu_custom_call" | custom-call | flops 30000000 | bytes 3000000 | tf_op jit(solution)/shard_map/weights/pallas_call | solution.py:138
  48.7 68.2 %all-to-all-done.1.rows_ref = f32[128,96,128]{2,1,0:T(8,128)} async-done(((f32[128,96,128]{2,1,0:T(8,128)}), f32[128,96,128]{2,1,0:T(8,128)}, u32[]{:S(2)}, u32[]{:S(2)}) %all-to-all-start.1) | async-done | bytes 6291488 | tf_op jit(solution)/shard_map/all_to_all | solution.py:194
  116.9 7.8 %pool.1 = f32[16,128,128]{2,1,0:T(8,128)} custom-call(bf16[16,128,768]{2,1,0:T(8,128)(2,1)} %weights.1.weight_ref, f32[128,96,128]{2,1,0:T(8,128)} %all-to-all-done.1.rows_ref), custom_call_target="tpu_custom_call" | custom-call | flops 20000000 | bytes 4000000 | tf_op jit(solution)/shard_map/pool/pallas_call | solution.py:167
  (6 shorter events, 0.1 us)
Async XLA Ops:
  0.0 0.9 copy-start
  3.3 21.1 %all-to-all-start = ((s32[8,2,384]{2,1,0:T(2,128)}), s32[8,2,384]{2,1,0:T(2,128)S(1)}, u32[]{:S(2)}, u32[]{:S(2)}) async-start(s32[8,2,384]{2,1,0:T(2,128)} %add_bitcast_fusion), calls=%async_computation | async-start | bytes 49152 | tf_op jit(solution)/shard_map/all_to_all | solution.py:204
  24.4 92.5 %all-to-all-start.1 = ((f32[128,96,128]{2,1,0:T(8,128)}), f32[128,96,128]{2,1,0:T(8,128)}, u32[]{:S(2)}, u32[]{:S(2)}) async-start(f32[128,96,128]{2,1,0:T(8,128)} %bitcast.21), calls=%async_computation.1 | async-start | bytes 12582912 | tf_op jit(solution)/shard_map/all_to_all | solution.py:194

commit v3 on v2

--- a/solution.py
+++ b/solution.py
@@ -191,17 +191,23 @@
     shard = row_shard.reshape(tables, lookups // LANES, LANES)
     offset = row_offset.reshape(tables, lookups // LANES, LANES).transpose(1, 0, 2)
     rows = front(mine.reshape(1), shard, offset.reshape(-1, LANES), table, blocks, cap)
+    rows, shard, bag_lengths = lax.optimization_barrier((rows, shard, bag_lengths))
     moved = lax.all_to_all(rows.reshape(blocks, tables * cap, width), AXES, 0, 0, tiled=True)
 
-    per_owner = (tables, groups, shards)
+    halves = look // LANES
     own = jnp.concatenate(
         [
-            lax.dynamic_index_in_dim(row_shard.reshape(*per_owner, look), mine, 2, keepdims=False),
-            lax.dynamic_index_in_dim(bag_lengths.reshape(*per_owner, bags), mine, 2, keepdims=False),
+            lax.dynamic_slice_in_dim(
+                shard.reshape(tables, groups, shards * halves, LANES), mine * halves, halves, 2
+            ).reshape(tables, groups, look),
+            lax.dynamic_index_in_dim(
+                bag_lengths.reshape(tables, groups, shards, bags), mine, 2, keepdims=False
+            ),
         ],
         axis=2,
     )
-    about = lax.all_to_all(own.transpose(1, 0, 2), "grp", 0, 0, tiled=True)
+    every = lax.all_gather(own, "grp")
+    about = lax.dynamic_index_in_dim(every, lax.axis_index("grp"), 2, keepdims=False)
     about = about.reshape(groups * tables, 1, look + bags)
     weights = make_weights(about[..., :look], about[..., look:], cap, shards)
     return pool(weights, moved, groups, cap)

time: 125 us -> 132 us (1.056)
  the two profiles are of different devices: /device:TPU:0 before, /device:TPU:51 now
where the time goes in v3:
time: 132 us
  blocking collectives  83.3 us (63%)
  Pallas kernels  35.4 us (27%)
  starting transfers between devices  10.8 us (8%)
  local copies, waits for them, and re-layouts  2.13 us (2%)
    all_gather x1, blocking collectives, body(): every = lax.all_gather(own, 'grp')  83.3 us
    pallas_call x1, Pallas kernels, front(): pl.pallas_call(functools.partial(front_kernel, tables, blocks, cap), out_...  16.6 us
    pallas_call x1, Pallas kernels, make_weights(): pl.pallas_call(functools.partial(weight_kernel, cap, shards), grid=(table...  11 us
    all_to_all x1, starting transfers between devices, body(): lax.all_to_all(rows.reshape(blocks, tables * cap, width), AXES, 0, 0, til...  10.8 us
    pallas_call x1, Pallas kernels, pool(): pl.pallas_call(functools.partial(pool_kernel, tables, cap), grid=(groups,...  7.83 us
  transfers between devices with their start and end apart: 1, of which 0 were waited for; matrix products, arithmetic and copies ran while one was open for 2% of the time, Pallas kernels for 8%

profile of v3, /device:TPU:51, one launch (start us, length us, event | category | flops | bytes accessed | tf_op | source)
XLA Modules:
  0.0 131.8 jit_solution(9293631995284538627)
XLA Ops:
  0.0 0.0 copy-start
  0.0 16.6 %front.1 = f32[12288,128]{1,0:T(8,128)} custom-call(s32[1]{0:T(128)} %bitcast.me_ref, s32[2,256,128]{2,1,0:T(8,128)} %bitcast.17, s32[512,128]{1,0:T(8,128)} %bitcast.19, f32[2,8192,128]{2,1,0:T(8,128)} %table_ref.1), custom_call_target="tpu_custom_call" | custom-call | flops 60000000 | bytes 15000000 | tf_op jit(solution)/shard_map/front/pallas_call | solution.py:85
  16.6 10.8 %all-to-all-start = ((f32[128,96,128]{2,1,0:T(8,128)}), f32[128,96,128]{2,1,0:T(8,128)}, u32[]{:S(2)}, u32[]{:S(2)}) async-start(f32[128,96,128]{2,1,0:T(8,128)} %bitcast.16), calls=%async_computation | async-start | bytes 12582912 | tf_op jit(solution)/shard_map/all_to_all | solution.py:195
  27.5 0.9 constant_dynamic-slice_fusion.2
  28.3 0.0 copy-done
  28.4 83.3 %all-gather = s32[16,8,384]{2,1,0:T(8,128)S(1)} all-gather(s32[2,8,384]{2,1,0:T(8,128)S(1)} %pad_add_fusion), channel_id=2, replica_groups=mesh['grp'=8,'row'=16] {'grp'}, dimensions={0}, use_global_device_ids=true | all-gather | bytes 221184 | tf_op jit(solution)/shard_map/all_gather | solution.py:209
  111.7 0.6 slice.9.length_ref
  112.3 0.6 slice.8.shard_ref
  112.9 11.0 %weights.1.weight_ref = bf16[16,128,768]{2,1,0:T(8,128)(2,1)} custom-call(s32[16,1,256]{2,1,0:T(1,128)} %slice.8.shard_ref, s32[16,1,128]{2,1,0:T(1,128)} %slice.9.length_ref), custom_call_target="tpu_custom_call" | custom-call | flops 30000000 | bytes 3000000 | tf_op jit(solution)/shard_map/weights/pallas_call | solution.py:138
  123.9 0.0 all-to-all-done.rows_ref
  123.9 7.8 %pool.1 = f32[16,128,128]{2,1,0:T(8,128)} custom-call(bf16[16,128,768]{2,1,0:T(8,128)(2,1)} %weights.1.weight_ref, f32[128,96,128]{2,1,0:T(8,128)} %all-to-all-done.rows_ref), custom_call_target="tpu_custom_call" | custom-call | flops 20000000 | bytes 4000000 | tf_op jit(solution)/shard_map/pool/pallas_call | solution.py:167
  (4 shorter events, 0.1 us)
Async XLA Ops:
  0.0 28.3 %copy-start = (s32[2,128,128]{2,1,0:T(8,128)S(1)}, s32[2,128,128]{2,1,0:T(8,128)}, u32[]{:S(2)}) copy-start(s32[2,128,128]{2,1,0:T(8,128)} %param.7) | copy-start | bytes 393220
  16.6 107.3 %all-to-all-start = ((f32[128,96,128]{2,1,0:T(8,128)}), f32[128,96,128]{2,1,0:T(8,128)}, u32[]{:S(2)}, u32[]{:S(2)}) async-start(f32[128,96,128]{2,1,0:T(8,128)} %bitcast.16), calls=%async_computation | async-start | bytes 12582912 | tf_op jit(solution)/shard_map/all_to_all | solution.py:195

commit v4 on v3

--- a/solution.py
+++ b/solution.py
@@ -13,25 +13,33 @@
 NT = (((1,), (1,)), ((), ()))
 VMEM_LIMIT = 56 * 1024 * 1024
 LANES = 128
-PIECES = 8
+FETCHES = 8
 
 
 def front_kernel(tables, blocks, cap, me_ref, shard_ref, offset_ref, table_ref, out_ref,
-                 key_s, off_s, list_v, list_s, held, rows, table_sem, list_sem, out_sem):
+                 key_s, off_s, list_v, held, rows, index_0, index_1, index_2, index_3,
+                 table_sem, list_sem, out_sem):
+    indices = (index_0, index_1, index_2, index_3)
     look = key_s.shape[0]
     halves = look // LANES
     size = table_ref.shape[1]
     me = me_ref[0]
-    fetch = [
-        pltpu.make_async_copy(table_ref.at[t], held.at[pl.ds(t * size, size)], table_sem.at[t])
-        for t in range(tables)
-    ]
+    part = tables * size // FETCHES
+    fetch = []
+    for i in range(FETCHES):
+        t, at = divmod(i * part, size)
+        fetch.append(
+            pltpu.make_async_copy(
+                table_ref.at[t, pl.ds(at, part)], held.at[pl.ds(i * part, part)], table_sem.at[i]
+            )
+        )
     for copy in fetch:
         copy.start()
     later = lax.broadcasted_iota(jnp.int32, (look, look), 0)
     earlier = lax.broadcasted_iota(jnp.int32, (look, look), 1)
     tri = (earlier < later).astype(F32).astype(BF16)
     places = [(lax.broadcasted_iota(jnp.int32, (8, blocks), 0) + 8 * i).astype(F32) for i in range(cap // 8)]
+    listed = []
     for t in range(tables):
         hit = jnp.concatenate(
             [(shard_ref[t, pl.ds(h, blocks, stride=halves), :] == me).astype(F32) for h in range(halves)], axis=1
@@ -49,34 +57,45 @@
                 accs = tuple(jnp.where(key == pos, off, acc) for acc, pos in zip(accs, places))
             return accs
 
-        accs = lax.fori_loop(0, look // 8, step, tuple(jnp.zeros((8, blocks), F32) for _ in places))
-        whole = jnp.concatenate(list(accs) + [jnp.zeros((LANES - cap, blocks), F32)], axis=0)
-        list_v[pl.ds(t * blocks, blocks), :] = jnp.transpose(whole).astype(jnp.int32)
-    listed = pltpu.make_async_copy(list_v, list_s, list_sem)
-    listed.start()
-    listed.wait()
+        listed += lax.fori_loop(0, look // 8, step, tuple(jnp.zeros((8, blocks), F32) for _ in places))
+    listed.append(jnp.zeros((LANES - tables * cap, blocks), F32))
+    list_v[...] = jnp.transpose(jnp.concatenate(listed, axis=0)).astype(jnp.int32)
+
+    per_block = tables * cap
+    per_tile = 8 * per_block
+    tiles = blocks // 8
+
+    def index_copy(tile, slot):
+        return pltpu.make_async_copy(list_v.at[pl.ds(tile * 8, 8)], indices[slot], list_sem.at[slot])
+
+    def out_copy(tile):
+        span = pl.ds(tile * per_tile, per_tile)
+        return pltpu.make_async_copy(rows.at[span], out_ref.at[span], out_sem.at[tile])
+
+    for slot in range(4):
+        index_copy(slot, slot).start()
     for copy in fetch:
         copy.wait()
 
-    per_piece = blocks // PIECES
-    per_block = tables * cap
-
-    def block(k, carry):
-        for t in range(tables):
-            for j in range(cap):
-                row = list_s[t * blocks + k, j]
-                rows[pl.ds(k * per_block + t * cap + j, 1), :] = held[pl.ds(row, 1), :]
+    def four(i, carry):
+        for slot in range(4):
+            tile = i * 4 + slot
+            index_copy(tile, slot).wait()
+            for u in range(8):
+                for j in range(per_block):
+                    row = indices[slot][u, j]
+                    rows[pl.ds(tile * per_tile + u * per_block + j, 1), :] = held[pl.ds(row, 1), :]
+            out_copy(tile).start()
+
+            @pl.when(tile + 4 < tiles)
+            def _():
+                index_copy(tile + 4, slot).start()
+
         return carry
 
-    sends = []
-    for i in range(PIECES):
-        lax.fori_loop(i * per_piece, (i + 1) * per_piece, block, 0)
-        part = pl.ds(i * per_piece * per_block, per_piece * per_block)
-        copy = pltpu.make_async_copy(rows.at[part], out_ref.at[part], out_sem.at[i])
-        copy.start()
-        sends.append(copy)
-    for copy in sends:
-        copy.wait()
+    lax.fori_loop(0, tiles // 4, four, 0)
+    for tile in range(tiles):
+        out_copy(tile).wait()
 
 
 def front(me, shard, offset, table, blocks, cap):
@@ -95,13 +114,15 @@
         scratch_shapes=[
             pltpu.VMEM((look, blocks), F32),
             pltpu.VMEM((look, blocks), F32),
-            pltpu.VMEM((tables * blocks, LANES), jnp.int32),
-            pltpu.SMEM((tables * blocks, LANES), jnp.int32),
+            pltpu.VMEM((blocks, LANES), jnp.int32),
             pltpu.VMEM((tables * size, width), F32),
             pltpu.VMEM((blocks * tables * cap, width), F32),
-            pltpu.SemaphoreType.DMA((tables,)),
-            pltpu.SemaphoreType.DMA,
-            pltpu.SemaphoreType.DMA((PIECES,)),
+        ]
+        + [pltpu.SMEM((8, LANES), jnp.int32)] * 4
+        + [
+            pltpu.SemaphoreType.DMA((FETCHES,)),
+            pltpu.SemaphoreType.DMA((4,)),
+            pltpu.SemaphoreType.DMA((blocks // 8,)),
         ],
         compiler_params=pltpu.CompilerParams(vmem_limit_bytes=VMEM_LIMIT),
         cost_estimate=pl.CostEstimate(flops=60_000_000, bytes_accessed=15_000_000, transcendentals=0),
@@ -144,35 +165,60 @@
             pl.BlockSpec((1, 1, bags), lambda i: (i, 0, 0)),
         ],
         out_specs=pl.BlockSpec((1, bags, shards * cap), lambda i: (i, 0, 0)),
+        compiler_params=pltpu.CompilerParams(vmem_limit_bytes=16 * 1024 * 1024),
         cost_estimate=pl.CostEstimate(flops=30_000_000, bytes_accessed=3_000_000, transcendentals=0),
         name="weights",
     )(shard, length)
 
 
-def pool_kernel(tables, cap, weight_ref, rows_ref, out_ref):
-    shards, _, width = rows_ref.shape
-    for t in range(tables):
-        rows = rows_ref[:, pl.ds(t * cap, cap), :].reshape(shards * cap, width)
-        high = rows.astype(BF16)
-        low = (rows - high.astype(F32)).astype(BF16)
-        both = jnp.dot(weight_ref[t], jnp.concatenate([high, low], axis=1), preferred_element_type=F32)
-        out_ref[t] = both[:, :width] + both[:, width:]
+def pool_kernel(groups, tables, cap, weight_ref, rows_ref, out_ref, rows_v, out_v, rows_sem, out_sem):
+    width = rows_v.shape[2]
+    shards = rows_v.shape[0] // groups
+
+    def rows_copy(g):
+        span = pl.ds(g * shards, shards)
+        return pltpu.make_async_copy(rows_ref.at[span], rows_v.at[span], rows_sem.at[g])
+
+    def out_copy(g):
+        span = pl.ds(g * tables, tables)
+        return pltpu.make_async_copy(out_v.at[span], out_ref.at[span], out_sem.at[g])
+
+    for g in range(groups):
+        rows_copy(g).start()
+
+    def group(g, carry):
+        rows_copy(g).wait()
+        for t in range(tables):
+            rows = rows_v[pl.ds(g * shards, shards), pl.ds(t * cap, cap), :].reshape(shards * cap, width)
+            high = rows.astype(BF16)
+            low = (rows - high.astype(F32)).astype(BF16)
+            both = jnp.dot(
+                weight_ref[g * tables + t], jnp.concatenate([high, low], axis=1), preferred_element_type=F32
+            )
+            out_v[g * tables + t] = both[:, :width] + both[:, width:]
+        out_copy(g).start()
+        return carry
+
+    lax.fori_loop(0, groups, group, 0)
+    for g in range(groups):
+        out_copy(g).wait()
 
 
 def pool(weights, rows, groups, cap):
-    total, bags, slots = weights.shape
-    tables = total // groups
-    shards = rows.shape[0] // groups
+    total, bags, _ = weights.shape
     width = rows.shape[2]
     return pl.pallas_call(
-        functools.partial(pool_kernel, tables, cap),
-        grid=(groups,),
+        functools.partial(pool_kernel, groups, total // groups, cap),
         out_shape=jax.ShapeDtypeStruct((total, bags, width), F32),
-        in_specs=[
-            pl.BlockSpec((tables, bags, slots), lambda i: (i, 0, 0)),
-            pl.BlockSpec((shards, tables * cap, width), lambda i: (i, 0, 0)),
-        ],
-        out_specs=pl.BlockSpec((tables, bags, width), lambda i: (i, 0, 0)),
+        in_specs=[pl.BlockSpec(memory_space=pltpu.VMEM), pl.BlockSpec(memory_space=pl.ANY)],
+        out_specs=pl.BlockSpec(memory_space=pl.ANY),
+        scratch_shapes=[
+            pltpu.VMEM(rows.shape, F32),
+            pltpu.VMEM((total, bags, width), F32),
+            pltpu.SemaphoreType.DMA((groups,)),
+            pltpu.SemaphoreType.DMA((groups,)),
+        ],
+        compiler_params=pltpu.CompilerParams(vmem_limit_bytes=40 * 1024 * 1024),
         cost_estimate=pl.CostEstimate(flops=20_000_000, bytes_accessed=4_000_000, transcendentals=0),
         name="pool",
     )(weights, rows)
@@ -191,7 +237,6 @@
     shard = row_shard.reshape(tables, lookups // LANES, LANES)
     offset = row_offset.reshape(tables, lookups // LANES, LANES).transpose(1, 0, 2)
     rows = front(mine.reshape(1), shard, offset.reshape(-1, LANES), table, blocks, cap)
-    rows, shard, bag_lengths = lax.optimization_barrier((rows, shard, bag_lengths))
     moved = lax.all_to_all(rows.reshape(blocks, tables * cap, width), AXES, 0, 0, tiled=True)
 
     halves = look // LANES
@@ -206,8 +251,7 @@
         ],
         axis=2,
     )
-    every = lax.all_gather(own, "grp")
-    about = lax.dynamic_index_in_dim(every, lax.axis_index("grp"), 2, keepdims=False)
+    about = lax.all_to_all(own.transpose(1, 0, 2), "grp", 0, 0, tiled=True)
     about = about.reshape(groups * tables, 1, look + bags)
     weights = make_weights(about[..., :look], about[..., look:], cap, shards)
     return pool(weights, moved, groups, cap)

time: 132 us -> 116 us (0.88)
  the two profiles are of different devices: /device:TPU:51 before, /device:TPU:0 now
where the time goes in v4:
time: 116 us
  waiting for transfers between devices  72.9 us (63%)
  Pallas kernels  23.8 us (21%)
  starting transfers between devices  16.4 us (14%)
  local copies, waits for them, and re-layouts  1.86 us (2%)
    all_to_all x1, waiting for transfers between devices, body(): lax.all_to_all(rows.reshape(blocks, tables * cap, width), AXES, 0, 0, til...  72.9 us
    pallas_call x1, Pallas kernels, front(): pl.pallas_call(functools.partial(front_kernel, tables, blocks, cap), out_...  12.2 us
    all_to_all x1, starting transfers between devices, body(): lax.all_to_all(rows.reshape(blocks, tables * cap, width), AXES, 0, 0, til...  12 us
    pallas_call x1, Pallas kernels, make_weights(): pl.pallas_call(functools.partial(weight_kernel, cap, shards), grid=(table...  7.44 us
    all_to_all x1, starting transfers between devices, body(): about = lax.all_to_all(own.transpose(1, 0, 2), 'grp', 0, 0, tiled=True)  4.41 us
    pallas_call x1, Pallas kernels, pool(): pl.pallas_call(functools.partial(pool_kernel, groups, total // groups, ca...  4.17 us
  transfers between devices with their start and end apart: 2, of which 1 were waited for; matrix products, arithmetic and copies ran while one was open for 0% of the time, Pallas kernels for 17%

profile of v4, /device:TPU:0, one launch (start us, length us, event | category | flops | bytes accessed | tf_op | source)
XLA Modules:
  0.0 115.7 jit_solution(16968739552286818126)
XLA Ops:
  0.0 0.0 copy-start
  0.0 0.9 copy-done
  0.9 0.9 constant_dynamic-slice_fusion.1
  1.8 0.6 add_bitcast_fusion
  2.4 4.4 %all-to-all-start = ((s32[8,2,384]{2,1,0:T(2,128)}), s32[8,2,384]{2,1,0:T(2,128)S(1)}, u32[]{:S(2)}, u32[]{:S(2)}) async-start(s32[8,2,384]{2,1,0:T(2,128)} %add_bitcast_fusion), calls=%async_computation | async-start | bytes 49152 | tf_op jit(solution)/shard_map/all_to_all | solution.py:254
  6.9 12.2 %front.1 = f32[12288,128]{1,0:T(8,128)} custom-call(s32[1]{0:T(128)} %bitcast.4.me_ref, s32[2,256,128]{2,1,0:T(8,128)} %bitcast.18, s32[512,128]{1,0:T(8,128)} %bitcast.19, f32[2,8192,128]{2,1,0:T(8,128)} %table_ref.1), custom_call_target="tpu_custom_call" | custom-call | flops 60000000 | bytes 15000000 | tf_op jit(solution)/shard_map/front/pallas_call | solution.py:104
  19.0 0.0 all-to-all-done
  19.0 12.0 %all-to-all-start.1 = ((f32[128,96,128]{2,1,0:T(8,128)}), f32[128,96,128]{2,1,0:T(8,128)}, u32[]{:S(2)}, u32[]{:S(2)}) async-start(f32[128,96,128]{2,1,0:T(8,128)} %bitcast.16), calls=%async_computation.1 | async-start | bytes 12582912 | tf_op jit(solution)/shard_map/all_to_all | solution.py:240
  31.1 7.4 %weights.1.weight_ref = bf16[16,128,768]{2,1,0:T(8,128)(2,1)S(1)} custom-call(s32[16,1,256]{2,1,0:T(1,128)S(1)} %slice.8.shard_ref, s32[16,1,128]{2,1,0:T(1,128)S(1)} %slice.9.length_ref), custom_call_target="tpu_custom_call" | custom-call | flops 30000000 | bytes 3000000 | tf_op jit(solution)/shard_map/weights/pallas_call | solution.py:159
  38.6 72.9 %all-to-all-done.1.rows_ref = f32[128,96,128]{2,1,0:T(8,128)} async-done(((f32[128,96,128]{2,1,0:T(8,128)}), f32[128,96,128]{2,1,0:T(8,128)}, u32[]{:S(2)}, u32[]{:S(2)}) %all-to-all-start.1) | async-done | bytes 6291488 | tf_op jit(solution)/shard_map/all_to_all | solution.py:240
  111.5 4.2 %pool.1 = f32[16,128,128]{2,1,0:T(8,128)} custom-call(bf16[16,128,768]{2,1,0:T(8,128)(2,1)S(1)} %weights.1.weight_ref, f32[128,96,128]{2,1,0:T(8,128)} %all-to-all-done.1.rows_ref), custom_call_target="tpu_custom_call" | custom-call | flops 20000000 | bytes 4000000 | tf_op jit(solution)/shard_map/pool/pallas_call | solution.py:210
  (7 shorter events, 0.1 us)
Async XLA Ops:
  0.0 0.9 copy-start
  2.4 16.6 %all-to-all-start = ((s32[8,2,384]{2,1,0:T(2,128)}), s32[8,2,384]{2,1,0:T(2,128)S(1)}, u32[]{:S(2)}, u32[]{:S(2)}) async-start(s32[8,2,384]{2,1,0:T(2,128)} %add_bitcast_fusion), calls=%async_computation | async-start | bytes 49152 | tf_op jit(solution)/shard_map/all_to_all | solution.py:254
  19.0 92.4 %all-to-all-start.1 = ((f32[128,96,128]{2,1,0:T(8,128)}), f32[128,96,128]{2,1,0:T(8,128)}, u32[]{:S(2)}, u32[]{:S(2)}) async-start(f32[128,96,128]{2,1,0:T(8,128)} %bitcast.16), calls=%async_computation.1 | async-start | bytes 12582912 | tf_op jit(solution)/shard_map/all_to_all | solution.py:240

commit v5 on v4

--- a/solution.py
+++ b/solution.py
@@ -8,6 +8,7 @@
 from jax.sharding import PartitionSpec as P
 
 AXES = ("grp", "row")
+MOVE = ("row", "grp")
 F32 = jnp.float32
 BF16 = jnp.bfloat16
 NT = (((1,), (1,)), ((), ()))
@@ -16,8 +17,8 @@
 FETCHES = 8
 
 
-def front_kernel(tables, blocks, cap, me_ref, shard_ref, offset_ref, table_ref, out_ref,
-                 key_s, off_s, list_v, held, rows, index_0, index_1, index_2, index_3,
+def front_kernel(tables, blocks, groups, cap, me_ref, shard_ref, offset_ref, table_ref, out_ref,
+                 key_s, off_s, by_block, list_v, held, rows, index_0, index_1, index_2, index_3,
                  table_sem, list_sem, out_sem):
     indices = (index_0, index_1, index_2, index_3)
     look = key_s.shape[0]
@@ -59,14 +60,16 @@
 
         listed += lax.fori_loop(0, look // 8, step, tuple(jnp.zeros((8, blocks), F32) for _ in places))
     listed.append(jnp.zeros((LANES - tables * cap, blocks), F32))
-    list_v[...] = jnp.transpose(jnp.concatenate(listed, axis=0)).astype(jnp.int32)
+    by_block[...] = jnp.transpose(jnp.concatenate(listed, axis=0)).astype(jnp.int32)
+    tiles = blocks // groups
+    for tile in range(tiles):
+        list_v[pl.ds(tile * groups, groups), :] = by_block[pl.ds(tile, groups, stride=tiles), :]
 
     per_block = tables * cap
-    per_tile = 8 * per_block
-    tiles = blocks // 8
+    per_tile = groups * per_block
 
     def index_copy(tile, slot):
-        return pltpu.make_async_copy(list_v.at[pl.ds(tile * 8, 8)], indices[slot], list_sem.at[slot])
+        return pltpu.make_async_copy(list_v.at[pl.ds(tile * groups, groups)], indices[slot], list_sem.at[slot])
 
     def out_copy(tile):
         span = pl.ds(tile * per_tile, per_tile)
@@ -74,35 +77,40 @@
 
     for slot in range(4):
         index_copy(slot, slot).start()
-    for copy in fetch:
-        copy.wait()
-
-    def four(i, carry):
-        for slot in range(4):
-            tile = i * 4 + slot
-            index_copy(tile, slot).wait()
-            for u in range(8):
-                for j in range(per_block):
-                    row = indices[slot][u, j]
-                    rows[pl.ds(tile * per_tile + u * per_block + j, 1), :] = held[pl.ds(row, 1), :]
-            out_copy(tile).start()
-
-            @pl.when(tile + 4 < tiles)
-            def _():
-                index_copy(tile + 4, slot).start()
-
-        return carry
-
-    lax.fori_loop(0, tiles // 4, four, 0)
+    for t in range(tables):
+        for i in range(t * FETCHES // tables, (t + 1) * FETCHES // tables):
+            fetch[i].wait()
+        last = t == tables - 1
+
+        def four(i, carry):
+            for slot in range(4):
+                tile = i * 4 + slot
+                index_copy(tile, slot).wait()
+                for u in range(groups):
+                    for j in range(t * cap, (t + 1) * cap):
+                        row = indices[slot][u, j]
+                        rows[pl.ds(tile * per_tile + u * per_block + j, 1), :] = held[pl.ds(row, 1), :]
+                if last:
+                    out_copy(tile).start()
+
+                    @pl.when(tile + 4 < tiles)
+                    def _():
+                        index_copy(tile + 4, slot).start()
+                else:
+                    index_copy(lax.rem(tile + 4, tiles), slot).start()
+
+            return carry
+
+        lax.fori_loop(0, tiles // 4, four, 0)
     for tile in range(tiles):
         out_copy(tile).wait()
 
 
-def front(me, shard, offset, table, blocks, cap):
+def front(me, shard, offset, table, blocks, groups, cap):
     tables, size, width = table.shape
     look = shard.shape[1] * LANES // blocks
     return pl.pallas_call(
-        functools.partial(front_kernel, tables, blocks, cap),
+        functools.partial(front_kernel, tables, blocks, groups, cap),
         out_shape=jax.ShapeDtypeStruct((blocks * tables * cap, width), F32),
         in_specs=[
             pl.BlockSpec(memory_space=pltpu.SMEM),
@@ -115,14 +123,15 @@
             pltpu.VMEM((look, blocks), F32),
             pltpu.VMEM((look, blocks), F32),
             pltpu.VMEM((blocks, LANES), jnp.int32),
+            pltpu.VMEM((blocks, LANES), jnp.int32),
             pltpu.VMEM((tables * size, width), F32),
             pltpu.VMEM((blocks * tables * cap, width), F32),
         ]
-        + [pltpu.SMEM((8, LANES), jnp.int32)] * 4
+        + [pltpu.SMEM((groups, LANES), jnp.int32)] * 4
         + [
             pltpu.SemaphoreType.DMA((FETCHES,)),
             pltpu.SemaphoreType.DMA((4,)),
-            pltpu.SemaphoreType.DMA((blocks // 8,)),
+            pltpu.SemaphoreType.DMA((blocks // groups,)),
         ],
         compiler_params=pltpu.CompilerParams(vmem_limit_bytes=VMEM_LIMIT),
         cost_estimate=pl.CostEstimate(flops=60_000_000, bytes_accessed=15_000_000, transcendentals=0),
@@ -172,12 +181,10 @@
 
 
 def pool_kernel(groups, tables, cap, weight_ref, rows_ref, out_ref, rows_v, out_v, rows_sem, out_sem):
-    width = rows_v.shape[2]
-    shards = rows_v.shape[0] // groups
+    _, shards, _, width = rows_v.shape
 
     def rows_copy(g):
-        span = pl.ds(g * shards, shards)
-        return pltpu.make_async_copy(rows_ref.at[span], rows_v.at[span], rows_sem.at[g])
+        return pltpu.make_async_copy(rows_ref.at[:, g], rows_v.at[g], rows_sem.at[g])
 
     def out_copy(g):
         span = pl.ds(g * tables, tables)
@@ -189,7 +196,7 @@
     def group(g, carry):
         rows_copy(g).wait()
         for t in range(tables):
-            rows = rows_v[pl.ds(g * shards, shards), pl.ds(t * cap, cap), :].reshape(shards * cap, width)
+            rows = rows_v[g, :, pl.ds(t * cap, cap), :].reshape(shards * cap, width)
             high = rows.astype(BF16)
             low = (rows - high.astype(F32)).astype(BF16)
             both = jnp.dot(
@@ -206,14 +213,14 @@
 
 def pool(weights, rows, groups, cap):
     total, bags, _ = weights.shape
-    width = rows.shape[2]
+    shards, _, slots, width = rows.shape
     return pl.pallas_call(
         functools.partial(pool_kernel, groups, total // groups, cap),
         out_shape=jax.ShapeDtypeStruct((total, bags, width), F32),
         in_specs=[pl.BlockSpec(memory_space=pltpu.VMEM), pl.BlockSpec(memory_space=pl.ANY)],
         out_specs=pl.BlockSpec(memory_space=pl.ANY),
         scratch_shapes=[
-            pltpu.VMEM(rows.shape, F32),
+            pltpu.VMEM((groups, shards, slots, width), F32),
             pltpu.VMEM((total, bags, width), F32),
             pltpu.SemaphoreType.DMA((groups,)),
             pltpu.SemaphoreType.DMA((groups,)),
@@ -236,8 +243,9 @@
 
     shard = row_shard.reshape(tables, lookups // LANES, LANES)
     offset = row_offset.reshape(tables, lookups // LANES, LANES).transpose(1, 0, 2)
-    rows = front(mine.reshape(1), shard, offset.reshape(-1, LANES), table, blocks, cap)
-    moved = lax.all_to_all(rows.reshape(blocks, tables * cap, width), AXES, 0, 0, tiled=True)
+    rows = front(mine.reshape(1), shard, offset.reshape(-1, LANES), table, blocks, groups, cap)
+    moved = lax.all_to_all(rows.reshape(blocks, tables * cap, width), MOVE, 0, 0, tiled=True)
+    moved = moved.reshape(shards, groups, tables * cap, width)
 
     halves = look // LANES
     own = jnp.concatenate(

time: 116 us -> 112 us (0.966)
  the two profiles are of different devices: /device:TPU:0 before, /device:TPU:27 now
where the time goes in v5:
time: 112 us
  waiting for transfers between devices  70.7 us (63%)
  Pallas kernels  22.9 us (20%)
  starting transfers between devices  15.7 us (14%)
  local copies, waits for them, and re-layouts  1.86 us (2%)
    all_to_all x1, waiting for transfers between devices, body(): lax.all_to_all(rows.reshape(blocks, tables * cap, width), MOVE, 0, 0, til...  70.7 us
    pallas_call x1, Pallas kernels, front(): pl.pallas_call(functools.partial(front_kernel, tables, blocks, groups, ca...  11.3 us
    all_to_all x1, starting transfers between devices, body(): lax.all_to_all(rows.reshape(blocks, tables * cap, width), MOVE, 0, 0, til...  10.6 us
    pallas_call x1, Pallas kernels, make_weights(): pl.pallas_call(functools.partial(weight_kernel, cap, shards), grid=(table...  7.44 us
    all_to_all x1, starting transfers between devices, body(): about = lax.all_to_all(own.transpose(1, 0, 2), 'grp', 0, 0, tiled=True)  5.11 us
    pallas_call x1, Pallas kernels, pool(): pl.pallas_call(functools.partial(pool_kernel, groups, total // groups, ca...  4.17 us
  transfers between devices with their start and end apart: 2, of which 1 were waited for; matrix products, arithmetic and copies ran while one was open for 0% of the time, Pallas kernels for 17%

profile of v5, /device:TPU:27, one launch (start us, length us, event | category | flops | bytes accessed | tf_op | source)
XLA Modules:
  0.0 111.8 jit_solution(15241562749887661176)
XLA Ops:
  0.0 0.0 copy-start
  0.0 0.9 copy-done
  0.9 0.9 constant_dynamic-slice_fusion.1
  1.8 0.6 add_bitcast_fusion
  2.4 5.1 %all-to-all-start = ((s32[8,2,384]{2,1,0:T(2,128)}), s32[8,2,384]{2,1,0:T(2,128)S(1)}, u32[]{:S(2)}, u32[]{:S(2)}) async-start(s32[8,2,384]{2,1,0:T(2,128)} %add_bitcast_fusion), calls=%async_computation | async-start | bytes 49152 | tf_op jit(solution)/shard_map/all_to_all | solution.py:262
  7.6 11.3 %front.1 = f32[12288,128]{1,0:T(8,128)} custom-call(s32[1]{0:T(128)} %bitcast.4.me_ref, s32[2,256,128]{2,1,0:T(8,128)} %bitcast.19, s32[512,128]{1,0:T(8,128)} %bitcast.20, f32[2,8192,128]{2,1,0:T(8,128)} %table_ref.1), custom_call_target="tpu_custom_call" | custom-call | flops 60000000 | bytes 15000000 | tf_op jit(solution)/shard_map/front/pallas_call | solution.py:112
  18.8 0.0 all-to-all-done
  18.8 10.6 %all-to-all-start.1 = ((f32[128,96,128]{2,1,0:T(8,128)}), f32[128,96,128]{2,1,0:T(8,128)}, u32[]{:S(2)}, u32[]{:S(2)}) async-start(f32[128,96,128]{2,1,0:T(8,128)} %bitcast.17), calls=%async_computation.1 | async-start | bytes 12582912 | tf_op jit(solution)/shard_map/all_to_all | solution.py:247
  29.5 7.4 %weights.1.weight_ref = bf16[16,128,768]{2,1,0:T(8,128)(2,1)S(1)} custom-call(s32[16,1,256]{2,1,0:T(1,128)S(1)} %slice.8.shard_ref, s32[16,1,128]{2,1,0:T(1,128)S(1)} %slice.9.length_ref), custom_call_target="tpu_custom_call" | custom-call | flops 30000000 | bytes 3000000 | tf_op jit(solution)/shard_map/weights/pallas_call | solution.py:168
  37.0 70.7 %all-to-all-done.1 = f32[128,96,128]{2,1,0:T(8,128)} async-done(((f32[128,96,128]{2,1,0:T(8,128)}), f32[128,96,128]{2,1,0:T(8,128)}, u32[]{:S(2)}, u32[]{:S(2)}) %all-to-all-start.1) | async-done | bytes 6291488 | tf_op jit(solution)/shard_map/all_to_all | solution.py:247
  107.7 4.2 %pool.1 = f32[16,128,128]{2,1,0:T(8,128)} custom-call(bf16[16,128,768]{2,1,0:T(8,128)(2,1)S(1)} %weights.1.weight_ref, f32[16,8,96,128]{3,2,1,0:T(8,128)} %bitcast.10.rows_ref), custom_call_target="tpu_custom_call" | custom-call | flops 20000000 | bytes 4000000 | tf_op jit(solution)/shard_map/pool/pallas_call | solution.py:217
  (7 shorter events, 0.1 us)
Async XLA Ops:
  0.0 0.9 copy-start
  2.4 16.4 %all-to-all-start = ((s32[8,2,384]{2,1,0:T(2,128)}), s32[8,2,384]{2,1,0:T(2,128)S(1)}, u32[]{:S(2)}, u32[]{:S(2)}) async-start(s32[8,2,384]{2,1,0:T(2,128)} %add_bitcast_fusion), calls=%async_computation | async-start | bytes 49152 | tf_op jit(solution)/shard_map/all_to_all | solution.py:262
  18.8 88.8 %all-to-all-start.1 = ((f32[128,96,128]{2,1,0:T(8,128)}), f32[128,96,128]{2,1,0:T(8,128)}, u32[]{:S(2)}, u32[]{:S(2)}) async-start(f32[128,96,128]{2,1,0:T(8,128)} %bitcast.17), calls=%async_computation.1 | async-start | bytes 12582912 | tf_op jit(solution)/shard_map/all_to_all | solution.py:247

commit v6 on v5

--- a/solution.py
+++ b/solution.py
@@ -15,6 +15,34 @@
 VMEM_LIMIT = 56 * 1024 * 1024
 LANES = 128
 FETCHES = 8
+AHEAD = 4
+
+
+def own_kernel(groups, me_ref, shard_ref, length_ref, out_ref):
+    tables, blocks, _ = length_ref.shape
+    halves = shard_ref.shape[1] // blocks
+    per_table = halves + 1
+    for g in range(groups):
+        k = me_ref[0] + g * (blocks // groups)
+        for t in range(tables):
+            for h in range(halves):
+                out_ref[g, pl.ds(t * per_table + h, 1), :] = shard_ref[t, pl.ds(k * halves + h, 1), :]
+            out_ref[g, pl.ds(t * per_table + halves, 1), :] = length_ref[t, pl.ds(k, 1), :]
+
+
+def own_blocks(me, shard, lengths, groups):
+    return pl.pallas_call(
+        functools.partial(own_kernel, groups),
+        out_shape=jax.ShapeDtypeStruct((groups, 8, LANES), jnp.int32),
+        in_specs=[
+            pl.BlockSpec(memory_space=pltpu.SMEM),
+            pl.BlockSpec(memory_space=pltpu.VMEM),
+            pl.BlockSpec(memory_space=pltpu.VMEM),
+        ],
+        out_specs=pl.BlockSpec(memory_space=pltpu.VMEM),
+        cost_estimate=pl.CostEstimate(flops=2_000_000, bytes_accessed=400_000, transcendentals=0),
+        name="own",
+    )(me, shard, lengths)
 
 
 def front_kernel(tables, blocks, groups, cap, me_ref, shard_ref, offset_ref, table_ref, out_ref,
@@ -34,7 +62,8 @@
                 table_ref.at[t, pl.ds(at, part)], held.at[pl.ds(i * part, part)], table_sem.at[i]
             )
         )
-    for copy in fetch:
+    early = FETCHES // tables
+    for copy in fetch[:early]:
         copy.start()
     later = lax.broadcasted_iota(jnp.int32, (look, look), 0)
     earlier = lax.broadcasted_iota(jnp.int32, (look, look), 1)
@@ -77,31 +106,38 @@
 
     for slot in range(4):
         index_copy(slot, slot).start()
-    for t in range(tables):
-        for i in range(t * FETCHES // tables, (t + 1) * FETCHES // tables):
-            fetch[i].wait()
-        last = t == tables - 1
-
-        def four(i, carry):
-            for slot in range(4):
-                tile = i * 4 + slot
-                index_copy(tile, slot).wait()
-                for u in range(groups):
-                    for j in range(t * cap, (t + 1) * cap):
-                        row = indices[slot][u, j]
-                        rows[pl.ds(tile * per_tile + u * per_block + j, 1), :] = held[pl.ds(row, 1), :]
-                if last:
-                    out_copy(tile).start()
-
-                    @pl.when(tile + 4 < tiles)
+    for copy in fetch[early:]:
+        copy.start()
+    spans = 2
+    fours = tiles // 4 // spans
+    span_step = 4 * fours
+    for span in range(spans):
+        for t in range(tables):
+            if span == 0:
+                for copy in fetch[t * early : (t + 1) * early]:
+                    copy.wait()
+            last = t == tables - 1
+
+            def four(i, carry):
+                for slot in range(4):
+                    tile = i * 4 + slot
+                    index_copy(tile, slot).wait()
+                    for u in range(groups):
+                        for j in range(t * cap, (t + 1) * cap):
+                            row = indices[slot][u, j]
+                            rows[pl.ds(tile * per_tile + u * per_block + j, 1), :] = held[pl.ds(row, 1), :]
+                    if last:
+                        out_copy(tile).start()
+                    again = span * span_step + slot + (span_step if last else 0)
+                    ahead = jnp.where(i + 1 < (span + 1) * fours, tile + 4, again)
+
+                    @pl.when(ahead < tiles)
                     def _():
-                        index_copy(tile + 4, slot).start()
-                else:
-                    index_copy(lax.rem(tile + 4, tiles), slot).start()
-
-            return carry
-
-        lax.fori_loop(0, tiles // 4, four, 0)
+                        index_copy(ahead, slot).start()
+
+                return carry
+
+            lax.fori_loop(span * fours, (span + 1) * fours, four, 0)
     for tile in range(tiles):
         out_copy(tile).wait()
 
@@ -139,45 +175,45 @@
     )(me, shard, offset, table)
 
 
-def weight_kernel(cap, shards, shard_ref, length_ref, out_ref):
-    look = shard_ref.shape[2]
-    bags = length_ref.shape[2]
-    shard = shard_ref[0].astype(F32)
-    ids = lax.broadcasted_iota(jnp.int32, (shards, look), 0).astype(F32)
-    hit = (shard == ids).astype(F32)
+def weight_kernel(tables, look, cap, shards, about_ref, out_ref):
+    bags = out_ref.shape[1]
+    halves = look // LANES
     row = lax.broadcasted_iota(jnp.int32, (look, look), 0)
     col = lax.broadcasted_iota(jnp.int32, (look, look), 1)
     upper = (row < col).astype(F32).astype(BF16)
-    before = jnp.dot(hit.astype(BF16), upper, preferred_element_type=F32)
-    slot = jnp.sum(hit * before, axis=0, keepdims=True) + shard * cap
+    ids = lax.broadcasted_iota(jnp.int32, (shards, look), 0).astype(F32)
     places = lax.broadcasted_iota(jnp.int32, (shards * cap, look), 0).astype(F32)
-    chosen = (places == slot).astype(F32).astype(BF16)
     brow = lax.broadcasted_iota(jnp.int32, (bags, bags), 0)
     bcol = lax.broadcasted_iota(jnp.int32, (bags, bags), 1)
-    length = length_ref[0].astype(F32)
-    ends = jnp.sum(jnp.where(bcol <= brow, length, 0.0), axis=1, keepdims=True)
-    starts = jnp.sum(jnp.where(bcol < brow, length, 0.0), axis=1, keepdims=True)
     spot = lax.broadcasted_iota(jnp.int32, (bags, look), 1).astype(F32)
-    inside = ((spot >= starts) & (spot < ends)).astype(F32).astype(BF16)
-    out_ref[0] = lax.dot_general(inside, chosen, NT, preferred_element_type=F32).astype(BF16)
-
-
-def make_weights(shard, length, cap, shards):
-    tables, _, look = shard.shape
-    bags = length.shape[2]
+    for t in range(tables):
+        first = t * (halves + 1)
+        shard = jnp.concatenate(
+            [about_ref[0, pl.ds(first + h, 1), :] for h in range(halves)], axis=1
+        ).astype(F32)
+        length = about_ref[0, pl.ds(first + halves, 1), :].astype(F32)
+        hit = (shard == ids).astype(F32)
+        before = jnp.dot(hit.astype(BF16), upper, preferred_element_type=F32)
+        slot = jnp.sum(hit * before, axis=0, keepdims=True) + shard * cap
+        chosen = (places == slot).astype(F32).astype(BF16)
+        ends = jnp.sum(jnp.where(bcol <= brow, length, 0.0), axis=1, keepdims=True)
+        starts = jnp.sum(jnp.where(bcol < brow, length, 0.0), axis=1, keepdims=True)
+        inside = ((spot >= starts) & (spot < ends)).astype(F32).astype(BF16)
+        out_ref[t] = lax.dot_general(inside, chosen, NT, preferred_element_type=F32).astype(BF16)
+
+
+def make_weights(about, tables, bags, look, cap, shards):
+    groups = about.shape[0]
     return pl.pallas_call(
-        functools.partial(weight_kernel, cap, shards),
-        grid=(tables,),
-        out_shape=jax.ShapeDtypeStruct((tables, bags, shards * cap), BF16),
-        in_specs=[
-            pl.BlockSpec((1, 1, look), lambda i: (i, 0, 0)),
-            pl.BlockSpec((1, 1, bags), lambda i: (i, 0, 0)),
-        ],
-        out_specs=pl.BlockSpec((1, bags, shards * cap), lambda i: (i, 0, 0)),
+        functools.partial(weight_kernel, tables, look, cap, shards),
+        grid=(groups,),
+        out_shape=jax.ShapeDtypeStruct((groups * tables, bags, shards * cap), BF16),
+        in_specs=[pl.BlockSpec((1, 8, LANES), lambda i: (i, 0, 0))],
+        out_specs=pl.BlockSpec((tables, bags, shards * cap), lambda i: (i, 0, 0)),
         compiler_params=pltpu.CompilerParams(vmem_limit_bytes=16 * 1024 * 1024),
         cost_estimate=pl.CostEstimate(flops=30_000_000, bytes_accessed=3_000_000, transcendentals=0),
         name="weights",
-    )(shard, length)
+    )(about)
 
 
 def pool_kernel(groups, tables, cap, weight_ref, rows_ref, out_ref, rows_v, out_v, rows_sem, out_sem):
@@ -190,10 +226,14 @@
         span = pl.ds(g * tables, tables)
         return pltpu.make_async_copy(out_v.at[span], out_ref.at[span], out_sem.at[g])
 
-    for g in range(groups):
+    for g in range(AHEAD):
         rows_copy(g).start()
 
     def group(g, carry):
+        @pl.when(g + AHEAD < groups)
+        def _():
+            rows_copy(g + AHEAD).start()
+
         rows_copy(g).wait()
         for t in range(tables):
             rows = rows_v[g, :, pl.ds(t * cap, cap), :].reshape(shards * cap, width)
@@ -247,21 +287,9 @@
     moved = lax.all_to_all(rows.reshape(blocks, tables * cap, width), MOVE, 0, 0, tiled=True)
     moved = moved.reshape(shards, groups, tables * cap, width)
 
-    halves = look // LANES
-    own = jnp.concatenate(
-        [
-            lax.dynamic_slice_in_dim(
-                shard.reshape(tables, groups, shards * halves, LANES), mine * halves, halves, 2
-            ).reshape(tables, groups, look),
-            lax.dynamic_index_in_dim(
-                bag_lengths.reshape(tables, groups, shards, bags), mine, 2, keepdims=False
-            ),
-        ],
-        axis=2,
-    )
-    about = lax.all_to_all(own.transpose(1, 0, 2), "grp", 0, 0, tiled=True)
-    about = about.reshape(groups * tables, 1, look + bags)
-    weights = make_weights(about[..., :look], about[..., look:], cap, shards)
+    own = own_blocks(mine.reshape(1), shard, bag_lengths, groups)
+    about = lax.all_to_all(own, "grp", 0, 0, tiled=True)
+    weights = make_weights(about, tables, bags, look, cap, shards)
     return pool(weights, moved, groups, cap)
 
 

time: 112 us -> 112 us (level)
  local copies, waits for them, and re-layouts: 1.86 us -> 0 us
  waiting for transfers between devices: 70.7 us -> 72.5 us
    all_to_all x1, waiting for transfers between devices: 70.7 us -> 72.5 us  [body(): lax.all_to_all(rows.reshape(blocks, tables * cap, width), MOVE, 0, 0, til...]
    pallas_call x1 -> x2, Pallas kernels: 7.44 us -> 7.3 us  [the longest x1 5.69 us: make_weights(): pl.pallas_call(functools.partial(weight_kernel, tables, look, cap, shards...]
  transfers between devices with their start and end apart: 2 -> 2, of which waited for: 1 -> 1; matrix products, arithmetic and copies ran while one was open for 0% -> 0% of each run, Pallas kernels for 17% -> 15%
where the time goes in v6:
time: 112 us; the launch traced here: 111 us
  waiting for transfers between devices  72.5 us (65%)
  Pallas kernels  22.9 us (20%)
  starting transfers between devices  15.7 us (14%)
    all_to_all x1, waiting for transfers between devices, body(): lax.all_to_all(rows.reshape(blocks, tables * cap, width), MOVE, 0, 0, til...  72.5 us
    pallas_call x1, Pallas kernels, front(): pl.pallas_call(functools.partial(front_kernel, tables, blocks, groups, ca...  11.2 us
    all_to_all x1, starting transfers between devices, body(): lax.all_to_all(rows.reshape(blocks, tables * cap, width), MOVE, 0, 0, til...  10.6 us
    pallas_call x1, Pallas kernels, make_weights(): pl.pallas_call(functools.partial(weight_kernel, tables, look, cap, shards...  5.69 us
    all_to_all x1, starting transfers between devices, body(): about = lax.all_to_all(own, 'grp', 0, 0, tiled=True)  5.11 us
    pallas_call x1, Pallas kernels, pool(): pl.pallas_call(functools.partial(pool_kernel, groups, total // groups, ca...  4.39 us
  transfers between devices with their start and end apart: 2, of which 1 were waited for; matrix products, arithmetic and copies ran while one was open for 0% of the time, Pallas kernels for 15%

profile of v6, /device:TPU:27, one launch (start us, length us, event | category | flops | bytes accessed | tf_op | source)
XLA Modules:
  0.0 111.2 jit_solution(14385905342064805023)
XLA Ops:
  0.0 1.6 %own.1 = s32[8,8,128]{2,1,0:T(8,128)} custom-call(s32[1]{0:T(128)} %bitcast.me_ref, s32[2,256,128]{2,1,0:T(8,128)} %bitcast.10, s32[2,128,128]{2,1,0:T(8,128)} %length_ref.1), custom_call_target="tpu_custom_call" | custom-call | flops 2000000 | bytes 400000 | tf_op jit(solution)/shard_map/own/pallas_call | solution.py:34
  1.6 5.1 %all-to-all-start = ((s32[8,8,128]{2,1,0:T(8,128)}), s32[8,8,128]{2,1,0:T(8,128)S(1)}, u32[]{:S(2)}, u32[]{:S(2)}) async-start(s32[8,8,128]{2,1,0:T(8,128)} %own.1), calls=%async_computation | async-start | bytes 65536 | tf_op jit(solution)/shard_map/all_to_all | solution.py:291
  6.7 11.2 %front.1 = f32[12288,128]{1,0:T(8,128)} custom-call(s32[1]{0:T(128)} %bitcast.me_ref, s32[2,256,128]{2,1,0:T(8,128)} %bitcast.11, s32[512,128]{1,0:T(8,128)} %bitcast.12, f32[2,8192,128]{2,1,0:T(8,128)} %table_ref.1), custom_call_target="tpu_custom_call" | custom-call | flops 60000000 | bytes 15000000 | tf_op jit(solution)/shard_map/front/pallas_call | solution.py:148
  18.0 0.0 all-to-all-done.about_ref
  18.0 10.6 %all-to-all-start.1 = ((f32[128,96,128]{2,1,0:T(8,128)}), f32[128,96,128]{2,1,0:T(8,128)}, u32[]{:S(2)}, u32[]{:S(2)}) async-start(f32[128,96,128]{2,1,0:T(8,128)} %bitcast.9), calls=%async_computation.1 | async-start | bytes 12582912 | tf_op jit(solution)/shard_map/all_to_all | solution.py:287
  28.6 5.7 %weights.1.weight_ref = bf16[16,128,768]{2,1,0:T(8,128)(2,1)S(1)} custom-call(s32[8,8,128]{2,1,0:T(8,128)S(1)} %all-to-all-done.about_ref), custom_call_target="tpu_custom_call" | custom-call | flops 30000000 | bytes 3000000 | tf_op jit(solution)/shard_map/weights/pallas_call | solution.py:207
  34.3 72.5 %all-to-all-done.1 = f32[128,96,128]{2,1,0:T(8,128)} async-done(((f32[128,96,128]{2,1,0:T(8,128)}), f32[128,96,128]{2,1,0:T(8,128)}, u32[]{:S(2)}, u32[]{:S(2)}) %all-to-all-start.1) | async-done | bytes 6291488 | tf_op jit(solution)/shard_map/all_to_all | solution.py:287
  106.9 4.4 %pool.1 = f32[16,128,128]{2,1,0:T(8,128)} custom-call(bf16[16,128,768]{2,1,0:T(8,128)(2,1)S(1)} %weights.1.weight_ref, f32[16,8,96,128]{3,2,1,0:T(8,128)} %bitcast.6.rows_ref), custom_call_target="tpu_custom_call" | custom-call | flops 20000000 | bytes 4000000 | tf_op jit(solution)/shard_map/pool/pallas_call | solution.py:257
Async XLA Ops:
  1.6 16.4 %all-to-all-start = ((s32[8,8,128]{2,1,0:T(8,128)}), s32[8,8,128]{2,1,0:T(8,128)S(1)}, u32[]{:S(2)}, u32[]{:S(2)}) async-start(s32[8,8,128]{2,1,0:T(8,128)} %own.1), calls=%async_computation | async-start | bytes 65536 | tf_op jit(solution)/shard_map/all_to_all | solution.py:291
  18.0 88.9 %all-to-all-start.1 = ((f32[128,96,128]{2,1,0:T(8,128)}), f32[128,96,128]{2,1,0:T(8,128)}, u32[]{:S(2)}, u32[]{:S(2)}) async-start(f32[128,96,128]{2,1,0:T(8,128)} %bitcast.9), calls=%async_computation.1 | async-start | bytes 12582912 | tf_op jit(solution)/shard_map/all_to_all | solution.py:287

commit v7 on v6

v7 whole, which is shorter than its diff:
```python
import functools

import jax
import jax.numpy as jnp
from jax import lax
from jax.experimental import pallas as pl
from jax.experimental.pallas import tpu as pltpu
from jax.sharding import PartitionSpec as P

AXES = ("grp", "row")
MOVE = ("row", "grp")
F32 = jnp.float32
BF16 = jnp.bfloat16
NT = (((1,), (1,)), ((), ()))
VMEM_LIMIT = 56 * 1024 * 1024
LANES = 128
FETCHES = 8


def front_kernel(tables, blocks, groups, cap, me_ref, shard_ref, offset_ref, length_ref, table_ref, out_ref,
                 key_s, off_s, end_s, by_block, meta_v, list_v, held, rows, index_0, index_1, index_2, index_3,
                 table_sem, list_sem, out_sem):
    indices = (index_0, index_1, index_2, index_3)
    look = key_s.shape[0]
    halves = look // LANES
    size = table_ref.shape[1]
    me = me_ref[0]
    part = tables * size // FETCHES
    fetch = []
    for i in range(FETCHES):
        t, at = divmod(i * part, size)
        fetch.append(
            pltpu.make_async_copy(
                table_ref.at[t, pl.ds(at, part)], held.at[pl.ds(i * part, part)], table_sem.at[i]
            )
        )
    early = FETCHES // tables
    for copy in fetch[:early]:
        copy.start()
    later = lax.broadcasted_iota(jnp.int32, (look, look), 0)
    earlier = lax.broadcasted_iota(jnp.int32, (look, look), 1)
    tri = (earlier < later).astype(F32).astype(BF16)
    places = [(lax.broadcasted_iota(jnp.int32, (8, blocks), 0) + 8 * i).astype(F32) for i in range(cap // 8)]
    bags = length_ref.shape[2]
    upto = lax.broadcasted_iota(jnp.int32, (bags, bags), 1) <= lax.broadcasted_iota(jnp.int32, (bags, bags), 0)
    upto = upto.astype(F32).astype(BF16)
    lane = lax.broadcasted_iota(jnp.int32, (blocks, LANES), 1)
    listed, bag_of = [], []
    for t in range(tables):
        hit = jnp.concatenate(
            [(shard_ref[t, pl.ds(h, blocks, stride=halves), :] == me).astype(F32) for h in range(halves)], axis=1
        )
        rank = lax.dot_general(tri, hit.astype(BF16), NT, preferred_element_type=F32)
        key_s[...] = jnp.where(jnp.transpose(hit) > 0.5, rank, -1.0)
        for h in range(halves):
            off = offset_ref[pl.ds(h * tables + t, blocks, stride=halves * tables), :] + t * size
            packed = off * look + (lane + h * LANES)
            off_s[pl.ds(h * LANES, LANES), :] = jnp.transpose(packed.astype(F32))
        end_s[...] = lax.dot_general(
            upto, length_ref[t].astype(F32).astype(BF16), NT, preferred_element_type=F32
        )

        def step(i, accs):
            for u in range(8):
                key = key_s[pl.ds(i * 8 + u, 1), :]
                off = off_s[pl.ds(i * 8 + u, 1), :]
                accs = tuple(jnp.where(key == pos, off, acc) for acc, pos in zip(accs, places))
            return accs

        found = lax.fori_loop(0, look // 8, step, tuple(jnp.full((8, blocks), -1.0, F32) for _ in places))
        found = [value.astype(jnp.int32) for value in found]
        spots = [(value & (look - 1)).astype(F32) for value in found]

        def count(i, accs):
            for u in range(8):
                end = end_s[pl.ds(i * 8 + u, 1), :]
                accs = tuple(acc + jnp.where(end <= spot, 1.0, 0.0) for acc, spot in zip(accs, spots))
            return accs

        counts = lax.fori_loop(0, bags // 8, count, tuple(jnp.zeros((8, blocks), F32) for _ in places))
        listed += [(jnp.maximum(value, 0) // look).astype(F32) for value in found]
        bag_of += [jnp.where(value >= 0, number, -1.0) for value, number in zip(found, counts)]
    spare = jnp.full((LANES - tables * cap, blocks), -1.0, F32)
    by_block[...] = jnp.transpose(jnp.concatenate(listed + [spare], axis=0)).astype(jnp.int32)
    turned = jnp.transpose(jnp.concatenate(bag_of + [spare], axis=0))
    meta_v[...] = pltpu.roll(turned, lax.rem(me * cap, LANES), 1)
    tiles = blocks // groups
    for tile in range(tiles):
        list_v[pl.ds(tile * groups, groups), :] = by_block[pl.ds(tile, groups, stride=tiles), :]
    per_block = tables * cap + 1
    per_tile = groups * per_block
    for tile in range(tiles):
        last_rows = pl.ds(tile * per_tile + per_block - 1, groups, stride=per_block)
        rows[last_rows, :] = meta_v[pl.ds(tile, groups, stride=tiles), :]

    def index_copy(tile, slot):
        return pltpu.make_async_copy(list_v.at[pl.ds(tile * groups, groups)], indices[slot], list_sem.at[slot])

    def out_copy(tile):
        span = pl.ds(tile * per_tile, per_tile)
        return pltpu.make_async_copy(rows.at[span], out_ref.at[span], out_sem.at[tile])

    for slot in range(4):
        index_copy(slot, slot).start()
    for copy in fetch[early:]:
        copy.start()
    spans = 2
    fours = tiles // 4 // spans
    span_step = 4 * fours
    for span in range(spans):
        for t in range(tables):
            if span == 0:
                for copy in fetch[t * early : (t + 1) * early]:
                    copy.wait()
            last = t == tables - 1

            def four(i, carry):
                for slot in range(4):
                    tile = i * 4 + slot
                    index_copy(tile, slot).wait()
                    for u in range(groups):
                        for j in range(t * cap, (t + 1) * cap):
                            row = indices[slot][u, j]
                            rows[pl.ds(tile * per_tile + u * per_block + j, 1), :] = held[pl.ds(row, 1), :]
                    if last:
                        out_copy(tile).start()
                    again = span * span_step + slot + (span_step if last else 0)
                    ahead = jnp.where(i + 1 < (span + 1) * fours, tile + 4, again)

                    @pl.when(ahead < tiles)
                    def _():
                        index_copy(ahead, slot).start()

                return carry

            lax.fori_loop(span * fours, (span + 1) * fours, four, 0)
    for tile in range(tiles):
        out_copy(tile).wait()


def front(me, shard, offset, lengths, table, blocks, groups, cap):
    tables, size, width = table.shape
    count = blocks * (tables * cap + 1)
    look = shard.shape[1] * LANES // blocks
    return pl.pallas_call(
        functools.partial(front_kernel, tables, blocks, groups, cap),
        out_shape=jax.ShapeDtypeStruct((count, width), F32),
        in_specs=[
            pl.BlockSpec(memory_space=pltpu.SMEM),
            pl.BlockSpec(memory_space=pltpu.VMEM),
            pl.BlockSpec(memory_space=pltpu.VMEM),
            pl.BlockSpec(memory_space=pltpu.VMEM),
            pl.BlockSpec(memory_space=pl.ANY),
        ],
        out_specs=pl.BlockSpec(memory_space=pl.ANY),
        scratch_shapes=[
            pltpu.VMEM((look, blocks), F32),
            pltpu.VMEM((look, blocks), F32),
            pltpu.VMEM((lengths.shape[2], blocks), F32),
            pltpu.VMEM((blocks, LANES), jnp.int32),
            pltpu.VMEM((blocks, LANES), F32),
            pltpu.VMEM((blocks, LANES), jnp.int32),
            pltpu.VMEM((tables * size, width), F32),
            pltpu.VMEM((count, width), F32),
        ]
        + [pltpu.SMEM((groups, LANES), jnp.int32)] * 4
        + [
            pltpu.SemaphoreType.DMA((FETCHES,)),
            pltpu.SemaphoreType.DMA((4,)),
            pltpu.SemaphoreType.DMA((blocks // groups,)),
        ],
        compiler_params=pltpu.CompilerParams(vmem_limit_bytes=VMEM_LIMIT),
        cost_estimate=pl.CostEstimate(flops=60_000_000, bytes_accessed=15_000_000, transcendentals=0),
        name="front",
    )(me, shard, offset, lengths, table)


def pool_kernel(groups, shards, tables, cap, rows_ref, out_ref, rows_v, out_v, rows_sem, out_sem):
    bags = out_v.shape[1]
    width = rows_v.shape[1]
    per_block = tables * cap + 1
    part = 2 * (per_block - 1) + 8

    def rows_copy(q, s):
        source = pl.ds((s * groups) * per_block + 2 * (per_block - 1) * q, part)
        target = pl.ds((q * shards + s) * part, part)
        return pltpu.make_async_copy(rows_ref.at[source], rows_v.at[target], rows_sem.at[q, s])

    def out_copy(g):
        span = pl.ds(g * tables, tables)
        return pltpu.make_async_copy(out_v.at[span], out_ref.at[span], out_sem.at[g])

    for q in range(groups // 2):
        for s in range(shards):
            rows_copy(q, s).start()
    numbers = lax.broadcasted_iota(jnp.int32, (bags, LANES), 0).astype(F32)
    lane = lax.broadcasted_iota(jnp.int32, (1, LANES), 1)
    for q in range(groups // 2):
        for s in range(shards):
            rows_copy(q, s).wait()

        def group(i, carry):
            g = 2 * q + i
            first = 2 * q + i * per_block
            start = q * shards * part + first
            meta = rows_v[pl.ds(start + per_block - 1, shards, stride=part), :]
            for t in range(tables):
                turned = meta if t == 0 else pltpu.roll(meta, LANES - t * cap, 1)
                weight = []
                for v in range(shards * cap // LANES):
                    low = v * LANES // cap
                    high = ((v + 1) * LANES - 1) // cap
                    bag = turned[low : low + 1, :]
                    for s in range(low + 1, high + 1):
                        bag = jnp.where(lane >= s * cap - v * LANES, turned[s : s + 1, :], bag)
                    weight.append((bag == numbers).astype(F32).astype(BF16))
                rows = jnp.concatenate(
                    [rows_v[pl.ds(start + s * part + t * cap, cap), :] for s in range(shards)], axis=0
                )
                high_part = rows.astype(BF16)
                low_part = (rows - high_part.astype(F32)).astype(BF16)
                both = jnp.dot(
                    jnp.concatenate(weight, axis=1),
                    jnp.concatenate([high_part, low_part], axis=1),
                    preferred_element_type=F32,
                )
                out_v[g * tables + t] = both[:, :width] + both[:, width:]
            out_copy(g).start()
            return carry

        lax.fori_loop(0, 2, group, 0)
    for g in range(groups):
        out_copy(g).wait()


def pool(rows, groups, shards, tables, bags, cap):
    width = rows.shape[1]
    part = 2 * tables * cap + 8
    return pl.pallas_call(
        functools.partial(pool_kernel, groups, shards, tables, cap),
        out_shape=jax.ShapeDtypeStruct((groups * tables, bags, width), F32),
        in_specs=[pl.BlockSpec(memory_space=pl.ANY)],
        out_specs=pl.BlockSpec(memory_space=pl.ANY),
        scratch_shapes=[
            pltpu.VMEM((groups // 2 * shards * part, width), F32),
            pltpu.VMEM((groups * tables, bags, width), F32),
            pltpu.SemaphoreType.DMA((groups // 2, shards)),
            pltpu.SemaphoreType.DMA((groups,)),
        ],
        compiler_params=pltpu.CompilerParams(vmem_limit_bytes=VMEM_LIMIT),
        cost_estimate=pl.CostEstimate(flops=20_000_000, bytes_accessed=8_000_000, transcendentals=0),
        name="pool",
    )(rows)


def body(table, row_shard, row_offset, bag_lengths):
    groups = lax.axis_size("grp")
    shards = lax.axis_size("row")
    mine = lax.axis_index("row")
    tables, _, width = table.shape
    blocks, bags = bag_lengths.shape[1:]
    lookups = row_offset.shape[1]
    look = lookups // blocks
    cap = 3 * look // shards

    shard = row_shard.reshape(tables, lookups // LANES, LANES)
    offset = row_offset.reshape(tables, lookups // LANES, LANES).transpose(1, 0, 2)
    offset = offset.reshape(-1, LANES)
    rows = front(mine.reshape(1), shard, offset, bag_lengths, table, blocks, groups, cap)
    moved = lax.all_to_all(rows.reshape(blocks, tables * cap + 1, 1, width), MOVE, 0, 0, tiled=True)
    return pool(moved.reshape(-1, width), groups, shards, tables, bags, cap)


def solution(mesh):
    placed = (P("grp", "row", None), P("grp", None, None), P("grp", None), P("grp", None, None))
    return jax.shard_map(
        body, mesh=mesh, in_specs=placed, out_specs=P(None, AXES, None), check_vma=False
    )
```

time: 112 us -> 105 us (0.938)
  the two profiles are of different devices: /device:TPU:27 before, /device:TPU:0 now
where the time goes in v7:
time: 105 us
  blocking collectives  87.3 us (83%)
  Pallas kernels  17.4 us (17%)
    all_to_all x1, blocking collectives, body(): lax.all_to_all(rows.reshape(blocks, tables * cap + 1, 1, width), MOVE, 0,...  87.3 us
    pallas_call x1, Pallas kernels, front(): pl.pallas_call(functools.partial(front_kernel, tables, blocks, groups, ca...  12.1 us
    pallas_call x1, Pallas kernels, pool(): pl.pallas_call(functools.partial(pool_kernel, groups, shards, tables, cap...  5.32 us

profile of v7, /device:TPU:0, one launch (start us, length us, event | category | flops | bytes accessed | tf_op | source)
XLA Modules:
  0.0 104.6 jit_solution(5516941810805948021)
XLA Ops:
  0.0 12.1 %front.1 = f32[12416,128]{1,0:T(8,128)} custom-call(s32[1]{0:T(128)} %bitcast.me_ref, s32[2,256,128]{2,1,0:T(8,128)} %bitcast.11, s32[512,128]{1,0:T(8,128)} %bitcast.12, s32[2,128,128]{2,1,0:T(8,128)} %length_ref.1, f32[2,8192,128]{2,1,0:T(8,128)} %table_ref.1), custom_call_target="tpu_custom_call" | custom-call | flops 60000000 | bytes 15000000 | tf_op jit(solution)/shard_map/front/pallas_call | solution.py:145
  12.1 87.3 %all_to_all.5 = f32[128,97,1,128]{3,2,1,0:T(1,128)} all-to-all(f32[128,97,1,128]{3,2,1,0:T(1,128)} %bitcast.10), channel_id=1, replica_groups=mesh['grp'=8,'row'=16] {'row','grp'}, dimensions={0} | all-to-all | bytes 12713984 | tf_op jit(solution)/shard_map/all_to_all | solution.py:270
  99.3 5.3 %pool.1 = f32[16,128,128]{2,1,0:T(8,128)} custom-call(f32[12416,128]{1,0:T(8,128)} %bitcast.9), custom_call_target="tpu_custom_call" | custom-call | flops 20000000 | bytes 8000000 | tf_op jit(solution)/shard_map/pool/pallas_call | solution.py:239

commit v8 on v7

--- a/solution.py
+++ b/solution.py
@@ -45,7 +45,13 @@
     upto = lax.broadcasted_iota(jnp.int32, (bags, bags), 1) <= lax.broadcasted_iota(jnp.int32, (bags, bags), 0)
     upto = upto.astype(F32).astype(BF16)
     lane = lax.broadcasted_iota(jnp.int32, (blocks, LANES), 1)
-    listed, bag_of = [], []
+    tiles = blocks // groups
+    bag_of = []
+
+    def index_copy(t, tile, slot):
+        source = list_v.at[pl.ds(t * blocks + tile * groups, groups)]
+        return pltpu.make_async_copy(source, indices[slot], list_sem.at[slot])
+
     for t in range(tables):
         hit = jnp.concatenate(
             [(shard_ref[t, pl.ds(h, blocks, stride=halves), :] == me).astype(F32) for h in range(halves)], axis=1
@@ -71,6 +77,18 @@
         found = [value.astype(jnp.int32) for value in found]
         spots = [(value & (look - 1)).astype(F32) for value in found]
 
+        spare = jnp.full((LANES - cap, blocks), -1.0, F32)
+        listed = [(jnp.maximum(value, 0) // look).astype(F32) for value in found]
+        by_block[...] = jnp.transpose(jnp.concatenate(listed + [spare], axis=0)).astype(jnp.int32)
+        for tile in range(tiles):
+            to = pl.ds(t * blocks + tile * groups, groups)
+            list_v[to, :] = by_block[pl.ds(tile, groups, stride=tiles), :]
+        if t == 0:
+            for slot in range(4):
+                index_copy(0, slot, slot).start()
+            for copy in fetch[early:]:
+                copy.start()
+
         def count(i, accs):
             for u in range(8):
                 end = end_s[pl.ds(i * 8 + u, 1), :]
@@ -78,32 +96,20 @@
             return accs
 
         counts = lax.fori_loop(0, bags // 8, count, tuple(jnp.zeros((8, blocks), F32) for _ in places))
-        listed += [(jnp.maximum(value, 0) // look).astype(F32) for value in found]
         bag_of += [jnp.where(value >= 0, number, -1.0) for value, number in zip(found, counts)]
     spare = jnp.full((LANES - tables * cap, blocks), -1.0, F32)
-    by_block[...] = jnp.transpose(jnp.concatenate(listed + [spare], axis=0)).astype(jnp.int32)
     turned = jnp.transpose(jnp.concatenate(bag_of + [spare], axis=0))
     meta_v[...] = pltpu.roll(turned, lax.rem(me * cap, LANES), 1)
-    tiles = blocks // groups
-    for tile in range(tiles):
-        list_v[pl.ds(tile * groups, groups), :] = by_block[pl.ds(tile, groups, stride=tiles), :]
     per_block = tables * cap + 1
     per_tile = groups * per_block
     for tile in range(tiles):
         last_rows = pl.ds(tile * per_tile + per_block - 1, groups, stride=per_block)
         rows[last_rows, :] = meta_v[pl.ds(tile, groups, stride=tiles), :]
 
-    def index_copy(tile, slot):
-        return pltpu.make_async_copy(list_v.at[pl.ds(tile * groups, groups)], indices[slot], list_sem.at[slot])
-
     def out_copy(tile):
         span = pl.ds(tile * per_tile, per_tile)
         return pltpu.make_async_copy(rows.at[span], out_ref.at[span], out_sem.at[tile])
 
-    for slot in range(4):
-        index_copy(slot, slot).start()
-    for copy in fetch[early:]:
-        copy.start()
     spans = 2
     fours = tiles // 4 // spans
     span_step = 4 * fours
@@ -117,19 +123,22 @@
             def four(i, carry):
                 for slot in range(4):
                     tile = i * 4 + slot
-                    index_copy(tile, slot).wait()
+                    index_copy(t, tile, slot).wait()
                     for u in range(groups):
-                        for j in range(t * cap, (t + 1) * cap):
+                        for j in range(cap):
                             row = indices[slot][u, j]
-                            rows[pl.ds(tile * per_tile + u * per_block + j, 1), :] = held[pl.ds(row, 1), :]
+                            at = tile * per_tile + u * per_block + t * cap + j
+                            rows[pl.ds(at, 1), :] = held[pl.ds(row, 1), :]
                     if last:
                         out_copy(tile).start()
+                    inside = i + 1 < (span + 1) * fours
                     again = span * span_step + slot + (span_step if last else 0)
-                    ahead = jnp.where(i + 1 < (span + 1) * fours, tile + 4, again)
+                    ahead = jnp.where(inside, tile + 4, again)
+                    table_ahead = jnp.where(inside, t, (t + 1) % tables)
 
                     @pl.when(ahead < tiles)
                     def _():
-                        index_copy(ahead, slot).start()
+                        index_copy(table_ahead, ahead, slot).start()
 
                 return carry
 
@@ -159,7 +168,7 @@
             pltpu.VMEM((lengths.shape[2], blocks), F32),
             pltpu.VMEM((blocks, LANES), jnp.int32),
             pltpu.VMEM((blocks, LANES), F32),
-            pltpu.VMEM((blocks, LANES), jnp.int32),
+            pltpu.VMEM((tables * blocks, LANES), jnp.int32),
             pltpu.VMEM((tables * size, width), F32),
             pltpu.VMEM((count, width), F32),
         ]
@@ -190,7 +199,7 @@
         span = pl.ds(g * tables, tables)
         return pltpu.make_async_copy(out_v.at[span], out_ref.at[span], out_sem.at[g])
 
-    for q in range(groups // 2):
+    for q in range(2):
         for s in range(shards):
             rows_copy(q, s).start()
     numbers = lax.broadcasted_iota(jnp.int32, (bags, LANES), 0).astype(F32)
@@ -198,6 +207,9 @@
     for q in range(groups // 2):
         for s in range(shards):
             rows_copy(q, s).wait()
+        if q + 2 < groups // 2:
+            for s in range(shards):
+                rows_copy(q + 2, s).start()
 
         def group(i, carry):
             g = 2 * q + i

time: 105 us -> 105 us (level)
  no operation moved by 1% of the time
where the time goes in v8:
time: 105 us
  blocking collectives  87.3 us (83%)
  Pallas kernels  17.3 us (16%)
    all_to_all x1, blocking collectives, body(): lax.all_to_all(rows.reshape(blocks, tables * cap + 1, 1, width), MOVE, 0,...  87.3 us
    pallas_call x1, Pallas kernels, front(): pl.pallas_call(functools.partial(front_kernel, tables, blocks, groups, ca...  11.7 us
    pallas_call x1, Pallas kernels, pool(): pl.pallas_call(functools.partial(pool_kernel, groups, shards, tables, cap...  5.6 us

profile of v8, /device:TPU:0, one launch (start us, length us, event | category | flops | bytes accessed | tf_op | source)
XLA Modules:
  0.0 104.6 jit_solution(9269573558447182456)
XLA Ops:
  0.0 11.7 %front.1 = f32[12416,128]{1,0:T(8,128)} custom-call(s32[1]{0:T(128)} %bitcast.me_ref, s32[2,256,128]{2,1,0:T(8,128)} %bitcast.11, s32[512,128]{1,0:T(8,128)} %bitcast.12, s32[2,128,128]{2,1,0:T(8,128)} %length_ref.1, f32[2,8192,128]{2,1,0:T(8,128)} %table_ref.1), custom_call_target="tpu_custom_call" | custom-call | flops 60000000 | bytes 15000000 | tf_op jit(solution)/shard_map/front/pallas_call | solution.py:154
  11.7 87.3 %all_to_all.5 = f32[128,97,1,128]{3,2,1,0:T(1,128)} all-to-all(f32[128,97,1,128]{3,2,1,0:T(1,128)} %bitcast.10), channel_id=1, replica_groups=mesh['grp'=8,'row'=16] {'row','grp'}, dimensions={0} | all-to-all | bytes 12713984 | tf_op jit(solution)/shard_map/all_to_all | solution.py:282
  99.0 5.6 %pool.1 = f32[16,128,128]{2,1,0:T(8,128)} custom-call(f32[12416,128]{1,0:T(8,128)} %bitcast.9), custom_call_target="tpu_custom_call" | custom-call | flops 20000000 | bytes 8000000 | tf_op jit(solution)/shard_map/pool/pallas_call | solution.py:251

commit v9 on v8

--- a/solution.py
+++ b/solution.py
@@ -15,12 +15,12 @@
 VMEM_LIMIT = 56 * 1024 * 1024
 LANES = 128
 FETCHES = 8
+SLOTS = 8
 
 
 def front_kernel(tables, blocks, groups, cap, me_ref, shard_ref, offset_ref, length_ref, table_ref, out_ref,
-                 key_s, off_s, end_s, by_block, meta_v, list_v, held, rows, index_0, index_1, index_2, index_3,
-                 table_sem, list_sem, out_sem):
-    indices = (index_0, index_1, index_2, index_3)
+                 key_s, off_s, end_s, by_block, meta_v, list_v, held, rows, *rest):
+    indices, (table_sem, list_sem, out_sem) = rest[:SLOTS], rest[SLOTS:]
     look = key_s.shape[0]
     halves = look // LANES
     size = table_ref.shape[1]
@@ -84,7 +84,7 @@
             to = pl.ds(t * blocks + tile * groups, groups)
             list_v[to, :] = by_block[pl.ds(tile, groups, stride=tiles), :]
         if t == 0:
-            for slot in range(4):
+            for slot in range(SLOTS):
                 index_copy(0, slot, slot).start()
             for copy in fetch[early:]:
                 copy.start()
@@ -110,39 +110,38 @@
         span = pl.ds(tile * per_tile, per_tile)
         return pltpu.make_async_copy(rows.at[span], out_ref.at[span], out_sem.at[tile])
 
-    spans = 2
-    fours = tiles // 4 // spans
-    span_step = 4 * fours
-    for span in range(spans):
-        for t in range(tables):
-            if span == 0:
-                for copy in fetch[t * early : (t + 1) * early]:
-                    copy.wait()
-            last = t == tables - 1
-
-            def four(i, carry):
-                for slot in range(4):
-                    tile = i * 4 + slot
-                    index_copy(t, tile, slot).wait()
-                    for u in range(groups):
-                        for j in range(cap):
-                            row = indices[slot][u, j]
-                            at = tile * per_tile + u * per_block + t * cap + j
-                            rows[pl.ds(at, 1), :] = held[pl.ds(row, 1), :]
-                    if last:
-                        out_copy(tile).start()
-                    inside = i + 1 < (span + 1) * fours
-                    again = span * span_step + slot + (span_step if last else 0)
-                    ahead = jnp.where(inside, tile + 4, again)
-                    table_ahead = jnp.where(inside, t, (t + 1) % tables)
-
-                    @pl.when(ahead < tiles)
+    rounds = tiles // SLOTS
+    for t in range(tables):
+        for copy in fetch[t * early : (t + 1) * early]:
+            copy.wait()
+        last = t == tables - 1
+
+        def several(i, carry):
+            for slot in range(SLOTS):
+                tile = i * SLOTS + slot
+                index_copy(t, tile, slot).wait()
+                for u in range(groups):
+                    for j in range(cap):
+                        row = indices[slot][u, j]
+                        at = tile * per_tile + u * per_block + t * cap + j
+                        rows[pl.ds(at, 1), :] = held[pl.ds(row, 1), :]
+                if last:
+                    out_copy(tile).start()
+                inside = i + 1 < rounds
+
+                @pl.when(inside)
+                def _():
+                    index_copy(t, tile + SLOTS, slot).start()
+
+                if not last:
+
+                    @pl.when(jnp.logical_not(inside))
                     def _():
-                        index_copy(table_ahead, ahead, slot).start()
-
-                return carry
-
-            lax.fori_loop(span * fours, (span + 1) * fours, four, 0)
+                        index_copy(t + 1, slot, slot).start()
+
+            return carry
+
+        lax.fori_loop(0, rounds, several, 0)
     for tile in range(tiles):
         out_copy(tile).wait()
 
@@ -172,10 +171,10 @@
             pltpu.VMEM((tables * size, width), F32),
             pltpu.VMEM((count, width), F32),
         ]
-        + [pltpu.SMEM((groups, LANES), jnp.int32)] * 4
+        + [pltpu.SMEM((groups, LANES), jnp.int32)] * SLOTS
         + [
             pltpu.SemaphoreType.DMA((FETCHES,)),
-            pltpu.SemaphoreType.DMA((4,)),
+            pltpu.SemaphoreType.DMA((SLOTS,)),
             pltpu.SemaphoreType.DMA((blocks // groups,)),
         ],
         compiler_params=pltpu.CompilerParams(vmem_limit_bytes=VMEM_LIMIT),
@@ -184,82 +183,63 @@
     )(me, shard, offset, lengths, table)
 
 
-def pool_kernel(groups, shards, tables, cap, rows_ref, out_ref, rows_v, out_v, rows_sem, out_sem):
+def pool_kernel(groups, shards, tables, cap, rows_ref, out_ref, out_v, out_sem):
     bags = out_v.shape[1]
-    width = rows_v.shape[1]
+    width = rows_ref.shape[1]
     per_block = tables * cap + 1
-    part = 2 * (per_block - 1) + 8
-
-    def rows_copy(q, s):
-        source = pl.ds((s * groups) * per_block + 2 * (per_block - 1) * q, part)
-        target = pl.ds((q * shards + s) * part, part)
-        return pltpu.make_async_copy(rows_ref.at[source], rows_v.at[target], rows_sem.at[q, s])
+    step = groups * per_block
 
     def out_copy(g):
         span = pl.ds(g * tables, tables)
         return pltpu.make_async_copy(out_v.at[span], out_ref.at[span], out_sem.at[g])
 
-    for q in range(2):
-        for s in range(shards):
-            rows_copy(q, s).start()
     numbers = lax.broadcasted_iota(jnp.int32, (bags, LANES), 0).astype(F32)
     lane = lax.broadcasted_iota(jnp.int32, (1, LANES), 1)
-    for q in range(groups // 2):
-        for s in range(shards):
-            rows_copy(q, s).wait()
-        if q + 2 < groups // 2:
-            for s in range(shards):
-                rows_copy(q + 2, s).start()
-
-        def group(i, carry):
-            g = 2 * q + i
-            first = 2 * q + i * per_block
-            start = q * shards * part + first
-            meta = rows_v[pl.ds(start + per_block - 1, shards, stride=part), :]
-            for t in range(tables):
-                turned = meta if t == 0 else pltpu.roll(meta, LANES - t * cap, 1)
-                weight = []
-                for v in range(shards * cap // LANES):
-                    low = v * LANES // cap
-                    high = ((v + 1) * LANES - 1) // cap
-                    bag = turned[low : low + 1, :]
-                    for s in range(low + 1, high + 1):
-                        bag = jnp.where(lane >= s * cap - v * LANES, turned[s : s + 1, :], bag)
-                    weight.append((bag == numbers).astype(F32).astype(BF16))
-                rows = jnp.concatenate(
-                    [rows_v[pl.ds(start + s * part + t * cap, cap), :] for s in range(shards)], axis=0
-                )
-                high_part = rows.astype(BF16)
-                low_part = (rows - high_part.astype(F32)).astype(BF16)
-                both = jnp.dot(
-                    jnp.concatenate(weight, axis=1),
-                    jnp.concatenate([high_part, low_part], axis=1),
-                    preferred_element_type=F32,
-                )
-                out_v[g * tables + t] = both[:, :width] + both[:, width:]
-            out_copy(g).start()
-            return carry
-
-        lax.fori_loop(0, 2, group, 0)
+
+    def group(g, carry):
+        start = g * per_block
+        meta = rows_ref[pl.ds(start + per_block - 1, shards, stride=step), :]
+        for t in range(tables):
+            turned = meta if t == 0 else pltpu.roll(meta, LANES - t * cap, 1)
+            weight = []
+            for v in range(shards * cap // LANES):
+                low = v * LANES // cap
+                high = ((v + 1) * LANES - 1) // cap
+                bag = turned[low : low + 1, :]
+                for s in range(low + 1, high + 1):
+                    bag = jnp.where(lane >= s * cap - v * LANES, turned[s : s + 1, :], bag)
+                weight.append((bag == numbers).astype(F32).astype(BF16))
+            rows = jnp.concatenate(
+                [rows_ref[pl.ds(start + s * step + t * cap, cap), :] for s in range(shards)], axis=0
+            )
+            high_part = rows.astype(BF16)
+            low_part = (rows - high_part.astype(F32)).astype(BF16)
+            both = jnp.dot(
+                jnp.concatenate(weight, axis=1),
+                jnp.concatenate([high_part, low_part], axis=1),
+                preferred_element_type=F32,
+            )
+            out_v[g * tables + t] = both[:, :width] + both[:, width:]
+        out_copy(g).start()
+        return carry
+
+    lax.fori_loop(0, groups, group, 0)
     for g in range(groups):
         out_copy(g).wait()
 
 
 def pool(rows, groups, shards, tables, bags, cap):
     width = rows.shape[1]
-    part = 2 * tables * cap + 8
     return pl.pallas_call(
         functools.partial(pool_kernel, groups, shards, tables, cap),
         out_shape=jax.ShapeDtypeStruct((groups * tables, bags, width), F32),
-        in_specs=[pl.BlockSpec(memory_space=pl.ANY)],
+        in_specs=[pl.BlockSpec(memory_space=pltpu.VMEM)],
         out_specs=pl.BlockSpec(memory_space=pl.ANY),
         scratch_shapes=[
-            pltpu.VMEM((groups // 2 * shards * part, width), F32),
             pltpu.VMEM((groups * tables, bags, width), F32),
-            pltpu.SemaphoreType.DMA((groups // 2, shards)),
             pltpu.SemaphoreType.DMA((groups,)),
         ],
-        compiler_params=pltpu.CompilerParams(vmem_limit_bytes=VMEM_LIMIT),
+        compiler_params=pltpu.CompilerParams(vmem_limit_bytes=16 * 1024 * 1024),
         cost_estimate=pl.CostEstimate(flops=20_000_000, bytes_accessed=8_000_000, transcendentals=0),
         name="pool",
     )(rows)

time: 105 us -> 106 us (level)
    pallas_call x1, Pallas kernels: 11.7 us -> 14.9 us  [front(): pl.pallas_call(functools.partial(front_kernel, tables, blocks, groups, ca...]
    pallas_call x1, Pallas kernels: 5.6 us -> 3.19 us  [pool(): pl.pallas_call(functools.partial(pool_kernel, groups, shards, tables, cap...]
where the time goes in v9:
time: 106 us; the launch traced here: 105 us
  blocking collectives  87.2 us (82%)
  Pallas kernels  18.1 us (17%)
    all_to_all x1, blocking collectives, body(): lax.all_to_all(rows.reshape(blocks, tables * cap + 1, 1, width), MOVE, 0,...  87.2 us
    pallas_call x1, Pallas kernels, front(): pl.pallas_call(functools.partial(front_kernel, tables, blocks, groups, ca...  14.9 us
    pallas_call x1, Pallas kernels, pool(): pl.pallas_call(functools.partial(pool_kernel, groups, shards, tables, cap...  3.19 us

profile of v9, /device:TPU:0, one launch (start us, length us, event | category | flops | bytes accessed | tf_op | source)
XLA Modules:
  0.0 105.3 jit_solution(16281031312039087682)
XLA Ops:
  0.0 14.9 %front.1 = f32[12416,128]{1,0:T(8,128)} custom-call(s32[1]{0:T(128)} %bitcast.me_ref, s32[2,256,128]{2,1,0:T(8,128)} %bitcast.11, s32[512,128]{1,0:T(8,128)} %bitcast.12, s32[2,128,128]{2,1,0:T(8,128)} %length_ref.1, f32[2,8192,128]{2,1,0:T(8,128)} %table_ref.1), custom_call_target="tpu_custom_call" | custom-call | flops 60000000 | bytes 15000000 | tf_op jit(solution)/shard_map/front/pallas_call | solution.py:153
  14.9 87.2 %all_to_all.5 = f32[128,97,1,128]{3,2,1,0:T(1,128)S(1)} all-to-all(f32[128,97,1,128]{3,2,1,0:T(1,128)} %bitcast.10), channel_id=1, replica_groups=mesh['grp'=8,'row'=16] {'row','grp'}, dimensions={0} | all-to-all | bytes 12713984 | tf_op jit(solution)/shard_map/all_to_all | solution.py:262
  102.1 3.2 %pool.1 = f32[16,128,128]{2,1,0:T(8,128)} custom-call(f32[12416,128]{1,0:T(8,128)S(1)} %bitcast.9), custom_call_target="tpu_custom_call" | custom-call | flops 20000000 | bytes 8000000 | tf_op jit(solution)/shard_map/pool/pallas_call | solution.py:233

commit v10 on v9

--- a/solution.py
+++ b/solution.py
@@ -15,12 +15,12 @@
 VMEM_LIMIT = 56 * 1024 * 1024
 LANES = 128
 FETCHES = 8
-SLOTS = 8
 
 
 def front_kernel(tables, blocks, groups, cap, me_ref, shard_ref, offset_ref, length_ref, table_ref, out_ref,
-                 key_s, off_s, end_s, by_block, meta_v, list_v, held, rows, *rest):
-    indices, (table_sem, list_sem, out_sem) = rest[:SLOTS], rest[SLOTS:]
+                 key_s, off_s, end_s, by_block, meta_v, list_v, held, rows, index_0, index_1, index_2, index_3,
+                 table_sem, list_sem, out_sem):
+    indices = (index_0, index_1, index_2, index_3)
     look = key_s.shape[0]
     halves = look // LANES
     size = table_ref.shape[1]
@@ -84,7 +84,7 @@
             to = pl.ds(t * blocks + tile * groups, groups)
             list_v[to, :] = by_block[pl.ds(tile, groups, stride=tiles), :]
         if t == 0:
-            for slot in range(SLOTS):
+            for slot in range(4):
                 index_copy(0, slot, slot).start()
             for copy in fetch[early:]:
                 copy.start()
@@ -110,38 +110,39 @@
         span = pl.ds(tile * per_tile, per_tile)
         return pltpu.make_async_copy(rows.at[span], out_ref.at[span], out_sem.at[tile])
 
-    rounds = tiles // SLOTS
-    for t in range(tables):
-        for copy in fetch[t * early : (t + 1) * early]:
-            copy.wait()
-        last = t == tables - 1
-
-        def several(i, carry):
-            for slot in range(SLOTS):
-                tile = i * SLOTS + slot
-                index_copy(t, tile, slot).wait()
-                for u in range(groups):
-                    for j in range(cap):
-                        row = indices[slot][u, j]
-                        at = tile * per_tile + u * per_block + t * cap + j
-                        rows[pl.ds(at, 1), :] = held[pl.ds(row, 1), :]
-                if last:
-                    out_copy(tile).start()
-                inside = i + 1 < rounds
-
-                @pl.when(inside)
-                def _():
-                    index_copy(t, tile + SLOTS, slot).start()
-
-                if not last:
-
-                    @pl.when(jnp.logical_not(inside))
+    spans = 2
+    fours = tiles // 4 // spans
+    span_step = 4 * fours
+    for span in range(spans):
+        for t in range(tables):
+            if span == 0:
+                for copy in fetch[t * early : (t + 1) * early]:
+                    copy.wait()
+            last = t == tables - 1
+
+            def four(i, carry):
+                for slot in range(4):
+                    tile = i * 4 + slot
+                    index_copy(t, tile, slot).wait()
+                    for u in range(groups):
+                        for j in range(cap):
+                            row = indices[slot][u, j]
+                            at = tile * per_tile + u * per_block + t * cap + j
+                            rows[pl.ds(at, 1), :] = held[pl.ds(row, 1), :]
+                    if last:
+                        out_copy(tile).start()
+                    inside = i + 1 < (span + 1) * fours
+                    again = span * span_step + slot + (span_step if last else 0)
+                    ahead = jnp.where(inside, tile + 4, again)
+                    table_ahead = jnp.where(inside, t, (t + 1) % tables)
+
+                    @pl.when(ahead < tiles)
                     def _():
-                        index_copy(t + 1, slot, slot).start()
-
-            return carry
-
-        lax.fori_loop(0, rounds, several, 0)
+                        index_copy(table_ahead, ahead, slot).start()
+
+                return carry
+
+            lax.fori_loop(span * fours, (span + 1) * fours, four, 0)
     for tile in range(tiles):
         out_copy(tile).wait()
 
@@ -171,10 +172,10 @@
             pltpu.VMEM((tables * size, width), F32),
             pltpu.VMEM((count, width), F32),
         ]
-        + [pltpu.SMEM((groups, LANES), jnp.int32)] * SLOTS
+        + [pltpu.SMEM((groups, LANES), jnp.int32)] * 4
         + [
             pltpu.SemaphoreType.DMA((FETCHES,)),
-            pltpu.SemaphoreType.DMA((SLOTS,)),
+            pltpu.SemaphoreType.DMA((4,)),
             pltpu.SemaphoreType.DMA((blocks // groups,)),
         ],
         compiler_params=pltpu.CompilerParams(vmem_limit_bytes=VMEM_LIMIT),

time: 106 us -> 103 us (0.972)
  Pallas kernels: 18.1 us -> 14.9 us
    pallas_call x1, Pallas kernels: 14.9 us -> 11.7 us  [front(): pl.pallas_call(functools.partial(front_kernel, tables, blocks, groups, ca...]
where the time goes in v10:
time: 103 us; the launch traced here: 102 us
  blocking collectives  87.2 us (85%)
  Pallas kernels  14.9 us (14%)
    all_to_all x1, blocking collectives, body(): lax.all_to_all(rows.reshape(blocks, tables * cap + 1, 1, width), MOVE, 0,...  87.2 us
    pallas_call x1, Pallas kernels, front(): pl.pallas_call(functools.partial(front_kernel, tables, blocks, groups, ca...  11.7 us
    pallas_call x1, Pallas kernels, pool(): pl.pallas_call(functools.partial(pool_kernel, groups, shards, tables, cap...  3.19 us

profile of v10, /device:TPU:0, one launch (start us, length us, event | category | flops | bytes accessed | tf_op | source)
XLA Modules:
  0.0 102.1 jit_solution(10752219316884345803)
XLA Ops:
  0.0 11.7 %front.1 = f32[12416,128]{1,0:T(8,128)} custom-call(s32[1]{0:T(128)} %bitcast.me_ref, s32[2,256,128]{2,1,0:T(8,128)} %bitcast.11, s32[512,128]{1,0:T(8,128)} %bitcast.12, s32[2,128,128]{2,1,0:T(8,128)} %length_ref.1, f32[2,8192,128]{2,1,0:T(8,128)} %table_ref.1), custom_call_target="tpu_custom_call" | custom-call | flops 60000000 | bytes 15000000 | tf_op jit(solution)/shard_map/front/pallas_call | solution.py:154
  11.7 87.2 %all_to_all.5 = f32[128,97,1,128]{3,2,1,0:T(1,128)S(1)} all-to-all(f32[128,97,1,128]{3,2,1,0:T(1,128)} %bitcast.10), channel_id=1, replica_groups=mesh['grp'=8,'row'=16] {'row','grp'}, dimensions={0} | all-to-all | bytes 12713984 | tf_op jit(solution)/shard_map/all_to_all | solution.py:263
  98.9 3.2 %pool.1 = f32[16,128,128]{2,1,0:T(8,128)} custom-call(f32[12416,128]{1,0:T(8,128)S(1)} %bitcast.9), custom_call_target="tpu_custom_call" | custom-call | flops 20000000 | bytes 8000000 | tf_op jit(solution)/shard_map/pool/pallas_call | solution.py:234

commit v11 on v10

--- a/solution.py
+++ b/solution.py
@@ -110,39 +110,39 @@
         span = pl.ds(tile * per_tile, per_tile)
         return pltpu.make_async_copy(rows.at[span], out_ref.at[span], out_sem.at[tile])
 
-    spans = 2
-    fours = tiles // 4 // spans
-    span_step = 4 * fours
-    for span in range(spans):
-        for t in range(tables):
-            if span == 0:
-                for copy in fetch[t * early : (t + 1) * early]:
-                    copy.wait()
-            last = t == tables - 1
-
-            def four(i, carry):
-                for slot in range(4):
-                    tile = i * 4 + slot
-                    index_copy(t, tile, slot).wait()
-                    for u in range(groups):
-                        for j in range(cap):
-                            row = indices[slot][u, j]
-                            at = tile * per_tile + u * per_block + t * cap + j
-                            rows[pl.ds(at, 1), :] = held[pl.ds(row, 1), :]
-                    if last:
-                        out_copy(tile).start()
-                    inside = i + 1 < (span + 1) * fours
-                    again = span * span_step + slot + (span_step if last else 0)
-                    ahead = jnp.where(inside, tile + 4, again)
-                    table_ahead = jnp.where(inside, t, (t + 1) % tables)
-
-                    @pl.when(ahead < tiles)
-                    def _():
-                        index_copy(table_ahead, ahead, slot).start()
-
-                return carry
-
-            lax.fori_loop(span * fours, (span + 1) * fours, four, 0)
+    fours = tiles // 4
+    for copy in fetch[:early]:
+        copy.wait()
+
+    def four(i, carry):
+        t = i // fours
+        quad = lax.rem(i, fours)
+
+        @pl.when(i == fours)
+        def _():
+            for copy in fetch[early:]:
+                copy.wait()
+
+        for slot in range(4):
+            tile = quad * 4 + slot
+            index_copy(t, tile, slot).wait()
+            for u in range(groups):
+                for j in range(cap):
+                    row = indices[slot][u, j]
+                    at = tile * per_tile + t * cap + (u * per_block + j)
+                    rows[pl.ds(at, 1), :] = held[pl.ds(row, 1), :]
+
+            @pl.when(t == tables - 1)
+            def _():
+                out_copy(tile).start()
+
+            @pl.when(i + 1 < tables * fours)
+            def _():
+                index_copy((i + 1) // fours, lax.rem(i + 1, fours) * 4 + slot, slot).start()
+
+        return carry
+
+    lax.fori_loop(0, tables * fours, four, 0)
     for tile in range(tiles):
         out_copy(tile).wait()
 

time: 103 us -> 103 us (level)
  no operation moved by 1% of the time
where the time goes in v11:
time: 103 us; the launch traced here: 102 us
  blocking collectives  87.2 us (85%)
  Pallas kernels  15 us (15%)
    all_to_all x1, blocking collectives, body(): lax.all_to_all(rows.reshape(blocks, tables * cap + 1, 1, width), MOVE, 0,...  87.2 us
    pallas_call x1, Pallas kernels, front(): pl.pallas_call(functools.partial(front_kernel, tables, blocks, groups, ca...  11.8 us
    pallas_call x1, Pallas kernels, pool(): pl.pallas_call(functools.partial(pool_kernel, groups, shards, tables, cap...  3.19 us

profile of v11, /device:TPU:0, one launch (start us, length us, event | category | flops | bytes accessed | tf_op | source)
XLA Modules:
  0.0 102.2 jit_solution(16702673875501891315)
XLA Ops:
  0.0 11.8 %front.1 = f32[12416,128]{1,0:T(8,128)} custom-call(s32[1]{0:T(128)} %bitcast.me_ref, s32[2,256,128]{2,1,0:T(8,128)} %bitcast.11, s32[512,128]{1,0:T(8,128)} %bitcast.12, s32[2,128,128]{2,1,0:T(8,128)} %length_ref.1, f32[2,8192,128]{2,1,0:T(8,128)} %table_ref.1), custom_call_target="tpu_custom_call" | custom-call | flops 60000000 | bytes 15000000 | tf_op jit(solution)/shard_map/front/pallas_call | solution.py:154
  11.8 87.2 %all_to_all.5 = f32[128,97,1,128]{3,2,1,0:T(1,128)S(1)} all-to-all(f32[128,97,1,128]{3,2,1,0:T(1,128)} %bitcast.10), channel_id=1, replica_groups=mesh['grp'=8,'row'=16] {'row','grp'}, dimensions={0} | all-to-all | bytes 12713984 | tf_op jit(solution)/shard_map/all_to_all | solution.py:263
  99.0 3.2 %pool.1 = f32[16,128,128]{2,1,0:T(8,128)} custom-call(f32[12416,128]{1,0:T(8,128)S(1)} %bitcast.9), custom_call_target="tpu_custom_call" | custom-call | flops 20000000 | bytes 8000000 | tf_op jit(solution)/shard_map/pool/pallas_call | solution.py:234

commit v12 on v11

--- a/solution.py
+++ b/solution.py
@@ -132,13 +132,13 @@
                     at = tile * per_tile + t * cap + (u * per_block + j)
                     rows[pl.ds(at, 1), :] = held[pl.ds(row, 1), :]
 
+            @pl.when(i + 1 < tables * fours)
+            def _():
+                index_copy((i + 1) // fours, lax.rem(i + 1, fours) * 4 + slot, slot).start()
+
             @pl.when(t == tables - 1)
             def _():
                 out_copy(tile).start()
-
-            @pl.when(i + 1 < tables * fours)
-            def _():
-                index_copy((i + 1) // fours, lax.rem(i + 1, fours) * 4 + slot, slot).start()
 
         return carry
 

time: 103 us -> 103 us (level)
  no operation moved by 1% of the time
where the time goes in v12:
time: 103 us; the launch traced here: 102 us
  blocking collectives  87.2 us (85%)
  Pallas kernels  15 us (15%)
    all_to_all x1, blocking collectives, body(): lax.all_to_all(rows.reshape(blocks, tables * cap + 1, 1, width), MOVE, 0,...  87.2 us
    pallas_call x1, Pallas kernels, front(): pl.pallas_call(functools.partial(front_kernel, tables, blocks, groups, ca...  11.8 us
    pallas_call x1, Pallas kernels, pool(): pl.pallas_call(functools.partial(pool_kernel, groups, shards, tables, cap...  3.19 us

profile of v12, /device:TPU:0, one launch (start us, length us, event | category | flops | bytes accessed | tf_op | source)
XLA Modules:
  0.0 102.2 jit_solution(7865170577041423752)
XLA Ops:
  0.0 11.8 %front.1 = f32[12416,128]{1,0:T(8,128)} custom-call(s32[1]{0:T(128)} %bitcast.me_ref, s32[2,256,128]{2,1,0:T(8,128)} %bitcast.11, s32[512,128]{1,0:T(8,128)} %bitcast.12, s32[2,128,128]{2,1,0:T(8,128)} %length_ref.1, f32[2,8192,128]{2,1,0:T(8,128)} %table_ref.1), custom_call_target="tpu_custom_call" | custom-call | flops 60000000 | bytes 15000000 | tf_op jit(solution)/shard_map/front/pallas_call | solution.py:154
  11.8 87.2 %all_to_all.5 = f32[128,97,1,128]{3,2,1,0:T(1,128)S(1)} all-to-all(f32[128,97,1,128]{3,2,1,0:T(1,128)} %bitcast.10), channel_id=1, replica_groups=mesh['grp'=8,'row'=16] {'row','grp'}, dimensions={0} | all-to-all | bytes 12713984 | tf_op jit(solution)/shard_map/all_to_all | solution.py:263
  99.0 3.2 %pool.1 = f32[16,128,128]{2,1,0:T(8,128)} custom-call(f32[12416,128]{1,0:T(8,128)S(1)} %bitcast.9), custom_call_target="tpu_custom_call" | custom-call | flops 20000000 | bytes 8000000 | tf_op jit(solution)/shard_map/pool/pallas_call | solution.py:234
